TPU v7x, 32 devices: a whole 2x2x4 slice. The times are simulated.
32 devices in a mesh: win: 2 (over y), dx: 4 (over z), dy: 2 (over x), dz: 2 (over core).
Axes of the slice: x: 2, y: 2, z: 4, core: 2. Of those that a mesh axis runs over, the one named last changes fastest.
Arguments:
- fraction: float32 [3, 8, 2, 2, 768], P(None, ('win', 'dx'), 'dy', 'dz'), parts along dimension 1, may hold values from 0 to 1
- atom_type: int32 [8, 2, 2, 768], P(('win', 'dx'), 'dy', 'dz'), parts along dimension 0, may hold values from 0 to 31
- perturbed: int32 [8, 2, 2, 768], P(('win', 'dx'), 'dy', 'dz'), parts along dimension 0, may hold values from 0 to 1
- leaving: int32 [8, 2, 2, 2, 16], P(('win', 'dx'), 'dy', 'dz'), parts along dimension 0, may hold values from 0 to 767, as said below
- neighbours: int32 [8, 2, 2, 6, 16], P(('win', 'dx'), 'dy', 'dz'), parts along dimension 0, may hold values from 0 to 161, as said below
- counts: int32 [8, 2, 2, 6], P(('win', 'dx'), 'dy', 'dz'), parts along dimension 0, may hold values from 1 to 16, as said below
- sigma_table: float32 [32], replicated, may hold values from 0.8 to 1.2
- depth_table: float32 [32], replicated, may hold values from 0.002 to 0.03
- charge_table: float32 [32], replicated, may hold values from -1 to 1
- domain_edge: float32 [3], replicated, may hold values from 1 to 1.12
- coupling: float32 [2], P('win'), parts along dimension 0, may hold values from 0.1 to 0.9
Outputs:
- forces: float32 [3, 8, 2, 2, 768], P(None, ('win', 'dx'), 'dy', 'dz'), parts along dimension 1
- energy: float32 [2], P('win'), parts along dimension 0
- dhdl: float32 [2], P('win'), parts along dimension 0
There are 2 independent parts, one for each index of `win`. A program takes and returns all parts, laid end to end along the dimension named above; an argument that names none is the same for every part. Nothing has to cross between parts.
Inputs may be any that keep to these rules, and one draw needn't show every extreme that they name: `leaving`: each domain lists 2 * 16 distinct slots: the first 16 leave toward the next domain, the last 16 toward the previous one. `neighbours`: each list holds 16 distinct ghost block numbers; entries at or past the block's count are valid numbers and are not used. `counts`: some block lists exactly 16 blocks in every draw.
All inputs are finite; a program needn't handle non-finite values.
Results may differ from a plain program's by a relative error of at most 0.0003.
Values sent between devices are 32-bit elements; how exact they have to be, the bound alone decides.
No kernel may reach another device: no remote copies, remote signals or barrier semaphores. Data moves between devices by JAX's collectives and lax.ppermute only.
A program may use at most 64 MiB of HBM per device.

v0:
```python
import jax
import jax.numpy as jnp
from jax import lax
from jax.sharding import PartitionSpec as P

soft_base = 0.3
soft_alpha = 0.5
charge_base = 0.3
charge_alpha = 0.5
coulomb = 0.1


def passed_along(array, axis, by):
    devices = lax.axis_size(axis)
    return lax.ppermute(array, axis, [(i, (i + by) % devices) for i in range(devices)])


def extended(block, sides, width):
    for axis, dim in sides:
        count = lax.axis_size(axis)
        forward = [(i, i + 1) for i in range(count - 1)]
        forward.append((count - 1, 0))
        backward = [(target, source) for source, target in forward]
        low = lax.ppermute(
            lax.slice_in_dim(block, block.shape[dim] - width, None, axis=dim), axis, forward
        )
        high = lax.ppermute(lax.slice_in_dim(block, 0, width, axis=dim), axis, backward)
        block = jnp.concatenate([low, block, high], axis=dim)
    return block


def swapped(block, axis, bit):
    count = lax.axis_size(axis)
    route = []
    for low in range(count):
        high = low | 1 << bit
        if high != low and high < count:
            route += [(low, high), (high, low)]
    return lax.ppermute(block, axis, route)


def lookup(table_row, type_ids):
    onehot = type_ids[None, :] == jnp.arange(table_row.shape[0], dtype=jnp.int32)[:, None]
    return jnp.sum(jnp.where(onehot, table_row[:, None], jnp.float32(0.0)), axis=0)


def pair_block(own_block, other_blocks, live_pairs, coupling_value):
    separation = own_block[0:3][None, :, :, None] - other_blocks[:, 0:3][:, :, None, :]
    radius_sq = jnp.sum(separation * separation, axis=1)
    sigma_pair = 0.5 * (own_block[3][None, :, None] + other_blocks[:, 3][:, None, :])
    depth_pair = jnp.sqrt(own_block[4][None, :, None] * other_blocks[:, 4][:, None, :])
    charges = own_block[5][None, :, None] * other_blocks[:, 5][:, None, :]
    flagged = jnp.maximum(own_block[6][None, :, None], other_blocks[:, 6][:, None, :])
    scaled = coupling_value * flagged
    sigma_two = sigma_pair * sigma_pair
    sigma_six = sigma_two * sigma_two * sigma_two
    soft_six = sigma_six * (soft_base + soft_alpha * scaled) + radius_sq * radius_sq * radius_sq
    soft_two = charge_base + charge_alpha * scaled + radius_sq
    inverse_six = 1.0 / soft_six
    energy_lj = (
        4.0
        * depth_pair
        * (sigma_six * sigma_six * inverse_six * inverse_six - sigma_six * inverse_six)
    )
    grad_six = (
        4.0
        * depth_pair
        * (
            sigma_six * inverse_six * inverse_six
            - 2.0 * sigma_six * sigma_six * inverse_six * inverse_six * inverse_six
        )
    )
    energy_coul = coulomb * charges * lax.rsqrt(soft_two)
    grad_two = -0.5 * energy_coul / soft_two
    weight = 1.0 - scaled
    total_pair = energy_lj + energy_coul
    pair_energy = jnp.sum(weight * total_pair * live_pairs)
    pair_dhdl = jnp.sum(
        flagged
        * (-total_pair + weight * (grad_six * sigma_six * soft_alpha + grad_two * charge_alpha))
        * live_pairs
    )
    force_scale = -weight * (6.0 * radius_sq * radius_sq * grad_six + 2.0 * grad_two) * live_pairs
    forces = jnp.sum(force_scale[:, None] * separation, axis=(0, 3))
    return (forces, pair_energy, pair_dhdl)


def block_terms(ghost_rows, listed_blocks, list_count, block_id, block_total, coupling_value):
    centre = 13 * block_total + block_id
    own_block = lax.dynamic_index_in_dim(ghost_rows, centre, 0, keepdims=False)
    other_blocks = jnp.take(ghost_rows, listed_blocks, axis=0)
    valid_slot = (jnp.arange(listed_blocks.shape[0], dtype=jnp.int32) < list_count).astype(
        jnp.float32
    )
    is_self = (listed_blocks == centre).astype(jnp.float32)[:, None, None] * jnp.eye(
        128, dtype=jnp.float32
    )[None]
    live_pairs = valid_slot[:, None, None] * (1.0 - is_self)
    return pair_block(own_block, other_blocks, live_pairs, coupling_value)


def on_device(
    fraction,
    atom_type,
    perturbed,
    leaving,
    neighbours,
    counts,
    sigma_table,
    depth_table,
    charge_table,
    domain_edge,
    coupling,
):
    atom_count = fraction.shape[-1]
    block_total = atom_count // 128
    spacing = float(atom_count) ** (1.0 / 3.0)
    type_ids = atom_type.reshape(atom_count)
    payload = jnp.concatenate(
        [
            fraction.reshape(3, atom_count),
            lookup(sigma_table, type_ids)[None],
            lookup(depth_table, type_ids)[None],
            lookup(charge_table, type_ids)[None],
            perturbed.reshape(1, atom_count).astype(jnp.float32),
        ],
        axis=0,
    )
    leave_slots = leaving.reshape(2, -1)
    shift_x = jnp.zeros((7, 1), jnp.float32).at[0].set(1.0)
    upward = payload[:, leave_slots[0]]
    downward = payload[:, leave_slots[1]]
    from_below = passed_along(upward, "dx", 1) - shift_x
    from_above = passed_along(downward, "dx", -1) + shift_x
    moved = payload.at[:, leave_slots[1]].set(from_below).at[:, leave_slots[0]].set(from_above)
    domain_block = moved.reshape(7, 1, 1, 1, atom_count)
    ghost_plane = extended(domain_block, (("dx", 1), ("dy", 2)), 1)
    partner = swapped(ghost_plane, "dz", 0)
    ghost_cells = jnp.concatenate([partner, ghost_plane, partner], axis=3)
    image_steps = jnp.arange(3, dtype=jnp.float32) - 1.0
    position = jnp.stack(
        [
            (ghost_cells[0] + image_steps[:, None, None, None]) * domain_edge[0] * spacing,
            (ghost_cells[1] + image_steps[None, :, None, None]) * domain_edge[1] * spacing,
            (ghost_cells[2] + image_steps[None, None, :, None]) * domain_edge[2] * spacing,
        ],
        axis=0,
    )
    ghost_all = jnp.concatenate([position, ghost_cells[3:]], axis=0)
    ghost_rows = (
        ghost_all.reshape(7, 27, block_total, 128)
        .transpose(1, 2, 0, 3)
        .reshape(27 * block_total, 7, 128)
    )
    listed = neighbours.reshape(block_total, -1)
    listed_count = counts.reshape(block_total)
    coupling_value = coupling[0]

    def one_block(block_id):
        return block_terms(
            ghost_rows,
            listed[block_id],
            listed_count[block_id],
            block_id,
            block_total,
            coupling_value,
        )

    forces, energies, dhdls = lax.map(one_block, jnp.arange(block_total, dtype=jnp.int32))
    forces = forces.transpose(1, 0, 2).reshape(3, 1, 1, 1, atom_count)
    window_energy, window_dhdl = lax.psum((jnp.sum(energies), jnp.sum(dhdls)), ("dx", "dy", "dz"))
    slot_total = jnp.float32(
        atom_count * lax.axis_size("dx") * lax.axis_size("dy") * lax.axis_size("dz")
    )
    energy = (0.5 * window_energy / slot_total).reshape(1)
    dhdl = (0.5 * window_dhdl / slot_total).reshape(1)
    return (forces, energy, dhdl)


def solution(mesh):
    return jax.shard_map(
        on_device,
        mesh=mesh,
        in_specs=(
            P(None, ("win", "dx"), "dy", "dz", None),
            P(("win", "dx"), "dy", "dz", None),
            P(("win", "dx"), "dy", "dz", None),
            P(("win", "dx"), "dy", "dz", None, None),
            P(("win", "dx"), "dy", "dz", None, None),
            P(("win", "dx"), "dy", "dz", None),
            P(),
            P(),
            P(),
            P(),
            P("win"),
        ),
        out_specs=(P(None, ("win", "dx"), "dy", "dz", None), P("win"), P("win")),
        check_vma=False,
    )
```

profile of v0, /device:TPU:0, one launch (start us, length us, event | category | flops | bytes accessed | tf_op | source)
XLA Modules:
  0.0 154.2 jit_solution(11909424343959024680)
XLA Ops:
  2.8 0.8 select_reduce_fusion
  5.1 3.1 %collective-permute-start = (f32[7,16]{0,1:T(8,128)S(1)}, f32[7,16]{0,1:T(8,128)S(1)}, u32[]{:S(2)}, u32[]{:S(2)}) collective-permute-start(f32[7,16]{0,1:T(8,128)S(1)} %bitcast.113), channel_id=1, source_target_pairs={{0,4},{4,8},{8,12},{12,0},{1,5},{5,9},{9,13},{13,1},{2,6},{6,10},{... | collective-permute-start | bytes 1352 | tf_op jit(solution)/shard_map/ppermute | solution.py:15
  8.8 2.1 %collective-permute-start.1 = (f32[7,16]{0,1:T(8,128)S(1)}, f32[7,16]{0,1:T(8,128)S(1)}, u32[]{:S(2)}, u32[]{:S(2)}) collective-permute-start(f32[7,16]{0,1:T(8,128)S(1)} %bitcast.112), channel_id=1, source_target_pairs={{0,12},{4,0},{8,4},{12,8},{1,13},{5,1},{9,5},{13,9},{2,14},{6,2},{... | collective-permute-start | bytes 1352 | tf_op jit(solution)/shard_map/ppermute | solution.py:15
  10.9 1.0 collective-permute-done
  11.9 0.9 scatter_custom_fusion
  12.9 0.8 scatter_custom_fusion.1
  13.7 3.5 %collective-permute-start.3 = (f32[7,1,1,1,768]{0,4,3,2,1:T(8,128)S(1)}, f32[7,1,1,1,768]{0,4,3,2,1:T(8,128)S(1)}, u32[]{:S(2)}, u32[]{:S(2)}) collective-permute-start(f32[7,1,1,1,768]{0,4,3,2,1:T(8,128)S(1)} %bitcast.97), channel_id=1, source_target_pairs={{4,0},{8,4},{12,8},{0,12},{5,1},{9,5},{13,9},{1,13},{6,2},{10,6},{... | collective-permute-start | bytes 64520 | tf_op jit(solution)/shard_map/ppermute | solution.py:27
  17.4 9.4 %collective-permute-done.3 = f32[7,1,1,1,768]{0,4,3,2,1:T(8,128)S(1)} collective-permute-done((f32[7,1,1,1,768]{0,4,3,2,1:T(8,128)S(1)}, f32[7,1,1,1,768]{0,4,3,2,1:T(8,128)S(1)}, u32[]{:S(2)}, u32[]{:S(2)}) %collective-permute-start.3) | collective-permute-done | bytes 21536 | tf_op jit(solution)/shard_map/ppermute | solution.py:27
  26.9 6.7 %collective-permute-done.2 = f32[7,1,1,1,768]{0,4,3,2,1:T(8,128)S(1)} collective-permute-done((f32[7,1,1,1,768]{0,4,3,2,1:T(8,128)S(1)}, f32[7,1,1,1,768]{0,4,3,2,1:T(8,128)S(1)}, u32[]{:S(2)}, u32[]{:S(2)}) %collective-permute-start.2) | collective-permute-done | bytes 21536 | tf_op jit(solution)/shard_map/ppermute | solution.py:24
  33.9 1.6 %collective-permute-start.5 = (f32[7,3,1,1,768]{4,3,2,1,0:T(1,128)S(1)}, f32[7,3,1,1,768]{4,3,2,1,0:T(1,128)S(1)}, u32[]{:S(2)}, u32[]{:S(2)}) collective-permute-start(f32[7,3,1,1,768]{4,3,2,1,0:T(1,128)S(1)} %pad_maximum_fusion.2), channel_id=1, source_target_pairs={{2,0},{0,2},{3,1},{1,3},{6,4},{4,6},{7,5},{5,7},{10,8},{8,10},{11,... | collective-permute-start | bytes 193544 | tf_op jit(solution)/shard_map/ppermute | solution.py:27
  36.0 2.2 %collective-permute-done.5 = f32[7,3,1,1,768]{4,3,2,1,0:T(1,128)S(1)} collective-permute-done((f32[7,3,1,1,768]{4,3,2,1,0:T(1,128)S(1)}, f32[7,3,1,1,768]{4,3,2,1,0:T(1,128)S(1)}, u32[]{:S(2)}, u32[]{:S(2)}) %collective-permute-start.5) | collective-permute-done | bytes 64544 | tf_op jit(solution)/shard_map/ppermute | solution.py:27
  38.2 1.5 collective-permute-done.4
  41.5 2.3 %fusion.34 = (f32[1,3,3,3,768]{4,0,3,2,1:T(1,128)S(1)}, f32[1,3,3,3,768]{4,0,3,2,1:T(1,128)S(1)}, f32[1,3,3,3,768]{4,0,3,2,1:T(1,128)S(1)}) fusion(f32[7,3,3,3,768]{4,0,3,2,1:T(8,128)S(1)} %copy_dynamic-update-slice_fusion.1, f32[3]{0:T(128)S(1)} %iota_add_fusion, f32[]{:T(128)} %bitcast.28, f32[]{:T(128)} %bitcast.32, f32[]{:T(128)} %bitcast.30), kind=kLoop, calls=%fused_computation.81 | loop fusion | flops 186624 | bytes 499212 | tf_op jit(solution)/shard_map/mul | solution.py:143
  44.2 72.7 %while.17 = (s32[]{:T(128)}, f32[6,3,128]{2,1,0:T(4,128)S(1)}, f32[6]{0:T(128)S(1)}, f32[6]{0:T(128)S(1)}, f32[]{:T(128)}, /*index=5*/s32[6]{0:T(128)S(1)}, f32[...) while((s32[]{:T(128)}, f32[6,3,128]{2,1,0:T(4,128)S(1)}, ...), condition=%wide.region_10.11_spmd, body=%wide.region_5.10_spmd.sunk | while | flops 20495192 | bytes 4781457 | solution.py:169
  50.5 3.8 %fusion.57 = (f32[]{:T(128)}, f32[]{:T(128)}, f32[16,128,128]{2,1,0:T(8,128)S(1)}) fusion(f32[128,128]{1,0:T(8,128)S(1)} %fusion.53, f32[16]{0:T(128)S(1)} %get-tuple-element.249, f32[16]{0:T(128)S(1)} %get-tuple-element.250, f32[16,128]{1,0:T(8,128)S(1)} %bitcast.104, f32[128]{0:T(128)S(1)} %get-tuple-element.253, f32[16,128]{1,0:T(8,128)S(1)} %bitcast.105, ...), kind=kLoop, calls=%fused_computation.33.clone.1 | loop fusion | flops 15990782 | bytes 2197644 | tf_op jit(solution)/shard_map/while/body/eval_jaxpr/reduce_sum | solution.py:78
  62.6 3.8 %fusion.57 = (f32[]{:T(128)}, f32[]{:T(128)}, f32[16,128,128]{2,1,0:T(8,128)S(1)}) fusion(f32[128,128]{1,0:T(8,128)S(1)} %fusion.53, f32[16]{0:T(128)S(1)} %get-tuple-element.249, f32[16]{0:T(128)S(1)} %get-tuple-element.250, f32[16,128]{1,0:T(8,128)S(1)} %bitcast.104, f32[128]{0:T(128)S(1)} %get-tuple-element.253, f32[16,128]{1,0:T(8,128)S(1)} %bitcast.105, ...), kind=kLoop, calls=%fused_computation.33.clone.1 | loop fusion | flops 15990782 | bytes 2197644 | tf_op jit(solution)/shard_map/while/body/eval_jaxpr/reduce_sum | solution.py:78
  66.9 0.8 dynamic_update_slice.25
  74.7 3.8 %fusion.57 = (f32[]{:T(128)}, f32[]{:T(128)}, f32[16,128,128]{2,1,0:T(8,128)S(1)}) fusion(f32[128,128]{1,0:T(8,128)S(1)} %fusion.53, f32[16]{0:T(128)S(1)} %get-tuple-element.249, f32[16]{0:T(128)S(1)} %get-tuple-element.250, f32[16,128]{1,0:T(8,128)S(1)} %bitcast.104, f32[128]{0:T(128)S(1)} %get-tuple-element.253, f32[16,128]{1,0:T(8,128)S(1)} %bitcast.105, ...), kind=kLoop, calls=%fused_computation.33.clone.1 | loop fusion | flops 15990782 | bytes 2197644 | tf_op jit(solution)/shard_map/while/body/eval_jaxpr/reduce_sum | solution.py:78
  79.0 0.8 dynamic_update_slice.25
  86.8 3.8 %fusion.57 = (f32[]{:T(128)}, f32[]{:T(128)}, f32[16,128,128]{2,1,0:T(8,128)S(1)}) fusion(f32[128,128]{1,0:T(8,128)S(1)} %fusion.53, f32[16]{0:T(128)S(1)} %get-tuple-element.249, f32[16]{0:T(128)S(1)} %get-tuple-element.250, f32[16,128]{1,0:T(8,128)S(1)} %bitcast.104, f32[128]{0:T(128)S(1)} %get-tuple-element.253, f32[16,128]{1,0:T(8,128)S(1)} %bitcast.105, ...), kind=kLoop, calls=%fused_computation.33.clone.1 | loop fusion | flops 15990782 | bytes 2197644 | tf_op jit(solution)/shard_map/while/body/eval_jaxpr/reduce_sum | solution.py:78
  98.9 3.8 %fusion.57 = (f32[]{:T(128)}, f32[]{:T(128)}, f32[16,128,128]{2,1,0:T(8,128)S(1)}) fusion(f32[128,128]{1,0:T(8,128)S(1)} %fusion.53, f32[16]{0:T(128)S(1)} %get-tuple-element.249, f32[16]{0:T(128)S(1)} %get-tuple-element.250, f32[16,128]{1,0:T(8,128)S(1)} %bitcast.104, f32[128]{0:T(128)S(1)} %get-tuple-element.253, f32[16,128]{1,0:T(8,128)S(1)} %bitcast.105, ...), kind=kLoop, calls=%fused_computation.33.clone.1 | loop fusion | flops 15990782 | bytes 2197644 | tf_op jit(solution)/shard_map/while/body/eval_jaxpr/reduce_sum | solution.py:78
  103.2 0.8 dynamic_update_slice.25
  111.1 3.8 %fusion.57 = (f32[]{:T(128)}, f32[]{:T(128)}, f32[16,128,128]{2,1,0:T(8,128)S(1)}) fusion(f32[128,128]{1,0:T(8,128)S(1)} %fusion.53, f32[16]{0:T(128)S(1)} %get-tuple-element.249, f32[16]{0:T(128)S(1)} %get-tuple-element.250, f32[16,128]{1,0:T(8,128)S(1)} %bitcast.104, f32[128]{0:T(128)S(1)} %get-tuple-element.253, f32[16,128]{1,0:T(8,128)S(1)} %bitcast.105, ...), kind=kLoop, calls=%fused_computation.33.clone.1 | loop fusion | flops 15990782 | bytes 2197644 | tf_op jit(solution)/shard_map/while/body/eval_jaxpr/reduce_sum | solution.py:78
  118.7 31.8 %all-reduce = (f32[]{:T(128)}, f32[]{:T(128)}) all-reduce(f32[]{:T(128)} %reduce_sum.96, f32[]{:T(128)} %reduce_sum.97), channel_id=1, replica_groups=mesh['win'=2,'dx'=4,'dy'=2,'dz'=2] {'dx','dy','dz'}, use_global_device_ids=true, to_apply=%region_12.13 | all-reduce | flops 2 | bytes 16 | tf_op jit(solution)/shard_map/psum | solution.py:171
  (151 shorter events, 36.6 us)
Async XLA Ops:
  0.6 12.2 %copy-start.2 = (f32[7]{0:T(128)S(1)}, f32[7]{0:T(128)}, u32[]{:S(2)}) copy-start(f32[7]{0:T(128)} %constant.159.clone.1) | copy-start | bytes 88
  5.1 6.8 %collective-permute-start = (f32[7,16]{0,1:T(8,128)S(1)}, f32[7,16]{0,1:T(8,128)S(1)}, u32[]{:S(2)}, u32[]{:S(2)}) collective-permute-start(f32[7,16]{0,1:T(8,128)S(1)} %bitcast.113), channel_id=1, source_target_pairs={{0,4},{4,8},{8,12},{12,0},{1,5},{5,9},{9,13},{13,1},{2,6},{6,10},{... | collective-permute-start | bytes 1352 | tf_op jit(solution)/shard_map/ppermute | solution.py:15
  8.8 27.1 %copy-start.1 = (s32[1,1,1,6,16]{4,2,3,1,0:T(1,128)S(1)}, s32[1,1,1,6,16]{4,2,3,1,0:T(1,128)}, u32[]{:S(2)}) copy-start(s32[1,1,1,6,16]{4,2,3,1,0:T(1,128)} %param.19) | copy-start | bytes 1156
  8.8 4.0 %collective-permute-start.1 = (f32[7,16]{0,1:T(8,128)S(1)}, f32[7,16]{0,1:T(8,128)S(1)}, u32[]{:S(2)}, u32[]{:S(2)}) collective-permute-start(f32[7,16]{0,1:T(8,128)S(1)} %bitcast.112), channel_id=1, source_target_pairs={{0,12},{4,0},{8,4},{12,8},{1,13},{5,1},{9,5},{13,9},{2,14},{6,2},{... | collective-permute-start | bytes 1352 | tf_op jit(solution)/shard_map/ppermute | solution.py:15
  12.8 27.1 %copy-start = (f32[3]{0:T(128)S(1)}, f32[3]{0:T(128)}, u32[]{:S(2)}) copy-start(f32[3]{0:T(128)} %param.24) | copy-start | bytes 40
  13.7 13.0 %collective-permute-start.3 = (f32[7,1,1,1,768]{0,4,3,2,1:T(8,128)S(1)}, f32[7,1,1,1,768]{0,4,3,2,1:T(8,128)S(1)}, u32[]{:S(2)}, u32[]{:S(2)}) collective-permute-start(f32[7,1,1,1,768]{0,4,3,2,1:T(8,128)S(1)} %bitcast.97), channel_id=1, source_target_pairs={{4,0},{8,4},{12,8},{0,12},{5,1},{9,5},{13,9},{1,13},{6,2},{10,6},{... | collective-permute-start | bytes 64520 | tf_op jit(solution)/shard_map/ppermute | solution.py:27
  17.2 16.4 %collective-permute-start.2 = (f32[7,1,1,1,768]{0,4,3,2,1:T(8,128)S(1)}, f32[7,1,1,1,768]{0,4,3,2,1:T(8,128)S(1)}, u32[]{:S(2)}, u32[]{:S(2)}) collective-permute-start(f32[7,1,1,1,768]{0,4,3,2,1:T(8,128)S(1)} %bitcast.98), channel_id=1, source_target_pairs={{0,4},{4,8},{8,12},{12,0},{1,5},{5,9},{9,13},{13,1},{2,6},{6,10},{... | collective-permute-start | bytes 64520 | tf_op jit(solution)/shard_map/ppermute | solution.py:24
  33.9 4.3 %collective-permute-start.5 = (f32[7,3,1,1,768]{4,3,2,1,0:T(1,128)S(1)}, f32[7,3,1,1,768]{4,3,2,1,0:T(1,128)S(1)}, u32[]{:S(2)}, u32[]{:S(2)}) collective-permute-start(f32[7,3,1,1,768]{4,3,2,1,0:T(1,128)S(1)} %pad_maximum_fusion.2), channel_id=1, source_target_pairs={{2,0},{0,2},{3,1},{1,3},{6,4},{4,6},{7,5},{5,7},{10,8},{8,10},{11,... | collective-permute-start | bytes 193544 | tf_op jit(solution)/shard_map/ppermute | solution.py:27
  35.4 4.3 %collective-permute-start.4 = (f32[7,3,1,1,768]{4,3,2,1,0:T(1,128)S(1)}, f32[7,3,1,1,768]{4,3,2,1,0:T(1,128)S(1)}, u32[]{:S(2)}, u32[]{:S(2)}) collective-permute-start(f32[7,3,1,1,768]{4,3,2,1,0:T(1,128)S(1)} %pad_maximum_fusion.2), channel_id=1, source_target_pairs={{0,2},{2,0},{1,3},{3,1},{4,6},{6,4},{5,7},{7,5},{8,10},{10,8},{9,1... | collective-permute-start | bytes 193544 | tf_op jit(solution)/shard_map/ppermute | solution.py:24
  39.8 1.5 collective-permute-start.6
  41.5 2.7 %copy-start.3 = (s32[1,1,1,6]{3,2,1,0:T(1,128)S(1)}, s32[1,1,1,6]{3,2,1,0:T(1,128)}, u32[]{:S(2)}) copy-start(s32[1,1,1,6]{3,2,1,0:T(1,128)} %param.20) | copy-start | bytes 76
where the time goes:
time: 155 us; the launch traced here: 154 us
  other arithmetic  41.6 us (27%)
  blocking collectives  31.8 us (21%)
  local copies, waits for them, and re-layouts  23.9 us (15%)
  waiting for transfers between devices  21.5 us (14%)
  loops' own time  20 us (13%)
  starting transfers between devices  10.9 us (7%)
  between operations  4.44 us (3%)
    psum x1, blocking collectives, on_device(): lax.psum((jnp.sum(energies), jnp.sum(dhdls)), ('dx', 'dy', 'dz'))  31.8 us
    reduce_sum x6, other arithmetic, pair_block(): jnp.sum(flagged * (-total_pair + weight * (grad_six * sigma_six * soft_al...  23.1 us
    another operation x1, loops' own time, on_device(): lax.map(one_block, jnp.arange(block_total, dtype=jnp.int32))  20 us
    ppermute x2, waiting for transfers between devices, extended(): lax.ppermute(lax.slice_in_dim(block, 0, width, axis=dim), axis, backward)  11.6 us
    dynamic_update_slice x18, local copies, waits for them, and re-layouts, on_device(): lax.map(one_block, jnp.arange(block_total, dtype=jnp.int32))  9.16 us
    ppermute x2, waiting for transfers between devices, extended(): lax.ppermute(lax.slice_in_dim(block, block.shape[dim] - width, None, axis...  8.23 us
    ppermute x2, starting transfers between devices, passed_along(): lax.ppermute(array, axis, [(i, (i + by) % devices) for i in range(devices)])  5.2 us
    ppermute x2, starting transfers between devices, extended(): lax.ppermute(lax.slice_in_dim(block, 0, width, axis=dim), axis, backward)  5.1 us
  transfers between devices with their start and end apart: 7, of which 6 were waited for; matrix products, arithmetic and copies ran while one was open for 2% of the time, Pallas kernels for 0%

commit v1 on v0

v1 whole, which is shorter than its diff:
```python
import functools

import jax
import jax.numpy as jnp
from jax import lax
from jax.experimental import pallas as pl
from jax.experimental.pallas import tpu as pltpu
from jax.sharding import PartitionSpec as P

soft_base = 0.3
soft_alpha = 0.5
charge_base = 0.3
charge_alpha = 0.5
coulomb = 0.1
LANES = 128
SUB = 8


def ring(count, by):
    return [((i + by) % count, i) for i in range(count)]


def grid_ring(count_y, count_z, by_y, by_z):
    route = []
    for y in range(count_y):
        for z in range(count_z):
            source = ((y + by_y) % count_y) * count_z + (z + by_z) % count_z
            route.append((source, y * count_z + z))
    return route


def gather_lanes(rows, lanes):
    return jnp.take_along_axis(rows, lanes, axis=1, mode="promise_in_bounds")


def pack_kernel(blocks, width, fraction, kind, flag, leaving, out, slab):
    slab[...] = jnp.zeros(slab.shape, jnp.float32)
    slab[0 : 3 * blocks, :] = fraction[...]
    slab[3 * blocks : 4 * blocks, :] = kind[...].astype(jnp.float32)
    slab[4 * blocks : 5 * blocks, :] = flag[...].astype(jnp.float32)
    head = slab.shape[0] - 2 * SUB
    slab[head : head + 1, 0:width] = leaving[...].astype(jnp.float32)
    slots = jnp.broadcast_to(slab[head : head + 1, :], (SUB, LANES)).astype(jnp.int32)
    lane = slots & (LANES - 1)
    block = slots >> 7
    here = lax.broadcasted_iota(jnp.int32, (SUB, LANES), 0) == block
    for k in range(5):
        picked = gather_lanes(slab[k * blocks : k * blocks + SUB, :], lane)
        picked = jnp.sum(jnp.where(here, picked, 0.0), axis=0, keepdims=True)
        slab[head + SUB + k : head + SUB + k + 1, :] = picked
    out[...] = slab[...]


def migrate_kernel(blocks, mig, below2, below, own, above, above2, out):
    pad = own.shape[0] - 2 * SUB
    tail = pad + SUB
    leavers = [
        below2[...],
        below[tail : tail + SUB, :],
        own[tail : tail + SUB, :],
        above[tail : tail + SUB, :],
        above2[...],
    ]
    lane = lax.broadcasted_iota(jnp.int32, (SUB, LANES), 1)
    row = lax.broadcasted_iota(jnp.int32, (SUB, LANES), 0)
    place = row * LANES + lane
    shift = jnp.where(row == 0, 1.0, 0.0)
    for d, base in enumerate((below, own, above)):
        slots = jnp.broadcast_to(base[pad : pad + 1, :], (SUB, LANES)).astype(jnp.int32)
        from_above = pltpu.roll(leavers[d + 2], LANES - mig, 1) + shift
        from_below = pltpu.roll(leavers[d], mig, 1) - shift
        incoming = jnp.where(lane < mig, from_above, from_below)
        origin = jnp.full((SUB, LANES), -1, jnp.int32)
        for m in range(2 * mig):
            spot = jnp.broadcast_to(slots[:, m : m + 1], (SUB, LANES))
            origin = jnp.where(place == spot, m, origin)
        arrives = origin >= 0
        source = jnp.maximum(origin, 0)
        for k in range(5):
            fresh = gather_lanes(jnp.broadcast_to(incoming[k : k + 1, :], (SUB, LANES)), source)
            held = base[k * blocks : k * blocks + SUB, :]
            kept = jnp.where(arrives, fresh, held)
            start = d * pad + k * blocks
            out[start : start + blocks, :] = kept[0:blocks]


def newton_reciprocal(x):
    guess = pl.reciprocal(x, approx=True)
    return guess * (2.0 - x * guess)


def pair_kernel(
    blocks, spacing, images, listed, counts, edge, coupling, sigma_t, depth_t, charge_t, *refs
):
    columns = refs[: max(c for c, _ in images) + 1]
    forces, sums = refs[len(columns) : len(columns) + 2]
    tables, ghost, staged, own, acc, turned = refs[len(columns) + 2 :]
    pad = columns[0].shape[0] // 3
    lam = coupling[0]
    types = sigma_t.shape[1]
    tables[0, :, 0:types] = jnp.broadcast_to(0.5 * sigma_t[...], (SUB, types))
    tables[1, :, 0:types] = jnp.broadcast_to(2.0 * jnp.sqrt(depth_t[...]), (SUB, types))
    tables[2, :, 0:types] = jnp.broadcast_to(charge_t[...], (SUB, types))
    for column in range(len(columns)):
        for a in range(3):
            part = [
                columns[column][a * pad + k * blocks : a * pad + k * blocks + SUB, :]
                for k in range(5)
            ]
            kind = part[3].astype(jnp.int32)
            fixed = [gather_lanes(tables[t], kind) for t in range(3)] + [part[4]]
            for where, (b, c) in images:
                if where != column:
                    continue
                at = (9 * a + 3 * b + c) * blocks
                for dim, step in enumerate((a, b, c)):
                    spot = (part[dim] + float(step - 1)) * edge[dim] * spacing
                    ghost[dim, at : at + blocks, :] = spot[0:blocks]
                for t in range(4):
                    ghost[3 + t, at : at + blocks, :] = fixed[t][0:blocks]
    centre = 13 * blocks
    staged[...] = jnp.zeros(staged.shape, jnp.float32)
    for k in range(7):
        staged[SUB * k : SUB * k + blocks, :] = ghost[k, centre : centre + blocks, :]
    columns_of = staged[...].T
    for q in range(blocks):
        for k in range(7):
            lane = SUB * k + q
            spread = jnp.broadcast_to(columns_of[:, lane : lane + 1], (LANES, LANES))
            if k == 5:
                spread = spread * coulomb
            own[q, k] = spread
            if k == 6:
                own[q, 7] = soft_base + soft_alpha * (lam * spread)
                own[q, 8] = 1.0 - lam * spread
    own_flag = staged[6 * SUB : 7 * SUB, :]
    own_eps = staged[4 * SUB : 5 * SUB, :]
    own_charge = staged[5 * SUB : 6 * SUB, :]
    self_a = soft_base + soft_alpha * (lam * own_flag)
    self_u = 1.0 / self_a
    self_t = own_eps * own_eps * self_u
    self_tu = self_t * self_u
    self_lj = self_tu - self_t
    self_rs = lax.rsqrt(self_a)
    self_c = coulomb * own_charge * own_charge * self_rs
    self_v = self_lj + self_c
    self_g = (self_lj + self_tu) * self_u + 0.5 * (self_c * (self_rs * self_rs))
    self_pv = own_flag * self_v
    self_pg = own_flag * self_g
    row = lax.broadcasted_iota(jnp.int32, (SUB, LANES), 0)
    lane_full = lax.broadcasted_iota(jnp.int32, (LANES, LANES), 1)
    turned[...] = jnp.zeros(turned.shape, jnp.float32)
    slots = listed.shape[0] // blocks

    def block(q, totals):
        acc[...] = jnp.zeros(acc.shape, jnp.float32)

        def entry(e, carry):
            sum_v, sum_pv, sum_pg, selves = carry
            h = listed[q * slots + e]
            other = [
                jnp.broadcast_to(ghost[k, pl.ds(h, 1), :], (SUB, LANES)) for k in range(7)
            ]
            other_a = soft_base + soft_alpha * (lam * other[6])
            other_w = 1.0 - lam * other[6]
            for g in range(LANES // SUB):
                at = slice(g * SUB, g * SUB + SUB)
                dx = own[q, 0, at, :] - other[0]
                dy = own[q, 1, at, :] - other[1]
                dz = own[q, 2, at, :] - other[2]
                r2 = dx * dx + dy * dy + dz * dz
                sigma = own[q, 3, at, :] + other[3]
                eps4 = own[q, 4, at, :] * other[4]
                qq = own[q, 5, at, :] * other[5]
                p = jnp.maximum(own[q, 6, at, :], other[6])
                a = jnp.maximum(own[q, 7, at, :], other_a)
                w = jnp.minimum(own[q, 8, at, :], other_w)
                s2 = sigma * sigma
                s6 = s2 * s2 * s2
                r4 = r2 * r2
                inv = newton_reciprocal(s6 * a + r4 * r2)
                rs = lax.rsqrt(a + r2)
                u = s6 * inv
                t = eps4 * u
                tu = t * u
                lj = tu - t
                k = lj + tu
                vc = qq * rs
                vcr = vc * (rs * rs)
                f = w * (vcr + 6.0 * (k * (r4 * inv)))
                acc[0, at, :] += f * dx
                acc[1, at, :] += f * dy
                acc[2, at, :] += f * dz
                v = lj + vc
                sum_v = sum_v + v
                sum_pv = sum_pv + p * v
                sum_pg = sum_pg + p * (k * u + 0.5 * vcr)
            return sum_v, sum_pv, sum_pg, selves + jnp.where(h == centre + q, 1.0, 0.0)

        sum_v, sum_pv, sum_pg, selves = lax.fori_loop(
            0, counts[q], entry, totals + (jnp.float32(0.0),)
        )
        held = jnp.where(row == q, selves, 0.0)
        for k in range(3):
            total = jnp.sum(acc[k], axis=1, keepdims=True)
            turned[...] = jnp.where(lane_full == k * blocks + q, total, turned[...])
        return (
            sum_v - held * self_v,
            sum_pv - held * self_pv,
            sum_pg - held * self_pg,
        )

    zero = jnp.zeros((SUB, LANES), jnp.float32)
    sum_v, sum_pv, sum_pg = lax.fori_loop(0, blocks, block, (zero, zero, zero))
    forces[...] = turned[...].T[0 : 3 * blocks, :]
    energy = sum_v - lam * sum_pv
    dhdl = -sum_pv - 0.5 * (1.0 - lam) * sum_pg
    energy = jnp.sum(jnp.sum(energy, axis=0, keepdims=True), axis=1, keepdims=True)
    dhdl = jnp.sum(jnp.sum(dhdl, axis=0, keepdims=True), axis=1, keepdims=True)
    lane = lax.broadcasted_iota(jnp.int32, (1, LANES), 1)
    sums[...] = jnp.where(lane == 0, energy, jnp.where(lane == 1, dhdl, 0.0))


def summed(value, axis):
    count = lax.axis_size(axis)
    if count & (count - 1):
        return lax.psum(value, axis)
    step = 1
    while step < count:
        value = value + lax.ppermute(value, axis, [(i, i ^ step) for i in range(count)])
        step *= 2
    return value


def on_device(
    fraction,
    atom_type,
    perturbed,
    leaving,
    neighbours,
    counts,
    sigma_table,
    depth_table,
    charge_table,
    domain_edge,
    coupling,
):
    atom_count = fraction.shape[-1]
    blocks = atom_count // LANES
    spacing = float(atom_count) ** (1.0 / 3.0)
    mig = leaving.shape[-1]
    types = sigma_table.shape[0]
    count_x, count_y, count_z = (lax.axis_size(axis) for axis in ("dx", "dy", "dz"))
    pad = -(-(5 * blocks + 2) // SUB) * SUB
    vmem = pl.BlockSpec(memory_space=pltpu.VMEM)
    smem = pl.BlockSpec(memory_space=pltpu.SMEM)
    packed = pl.pallas_call(
        functools.partial(pack_kernel, blocks, 2 * mig),
        in_specs=[vmem] * 4,
        out_specs=vmem,
        out_shape=jax.ShapeDtypeStruct((pad + 2 * SUB, LANES), jnp.float32),
        scratch_shapes=[pltpu.VMEM((pad + 2 * SUB, LANES), jnp.float32)],
        name="pack",
    )(
        fraction.reshape(3 * blocks, LANES),
        atom_type.reshape(blocks, LANES),
        perturbed.reshape(blocks, LANES),
        leaving.reshape(1, 2 * mig),
    )
    below = lax.ppermute(packed, "dx", ring(count_x, -1))
    above = lax.ppermute(packed, "dx", ring(count_x, 1))
    leavers = packed[pad + SUB :]
    below2 = lax.ppermute(leavers, "dx", ring(count_x, -2))
    if (count_x - 2) % count_x == 2 % count_x:
        above2 = below2
    else:
        above2 = lax.ppermute(leavers, "dx", ring(count_x, 2))
    moved = pl.pallas_call(
        functools.partial(migrate_kernel, blocks, mig),
        in_specs=[vmem] * 5,
        out_specs=vmem,
        out_shape=jax.ShapeDtypeStruct((3 * pad, LANES), jnp.float32),
        name="migrate",
    )(below2, below, packed, above, above2)
    places, columns, images = {(0, 0): 0}, [moved], []
    for b in range(3):
        for c in range(3):
            key = ((b - 1) % count_y, (c - 1) % count_z)
            if key not in places:
                places[key] = len(columns)
                columns.append(
                    lax.ppermute(moved, ("dy", "dz"), grid_ring(count_y, count_z, *key))
                )
            images.append((places[key], (b, c)))
    rows = -(-27 * blocks // SUB) * SUB
    forces, sums = pl.pallas_call(
        functools.partial(pair_kernel, blocks, spacing, images),
        in_specs=[smem] * 4 + [vmem] * (3 + len(columns)),
        out_specs=[vmem, vmem],
        out_shape=[
            jax.ShapeDtypeStruct((3 * blocks, LANES), jnp.float32),
            jax.ShapeDtypeStruct((1, LANES), jnp.float32),
        ],
        scratch_shapes=[
            pltpu.VMEM((3, SUB, LANES), jnp.float32),
            pltpu.VMEM((7, rows, LANES), jnp.float32),
            pltpu.VMEM((LANES, LANES), jnp.float32),
            pltpu.VMEM((blocks, 9, LANES, LANES), jnp.float32),
            pltpu.VMEM((3, LANES, LANES), jnp.float32),
            pltpu.VMEM((LANES, LANES), jnp.float32),
        ],
        name="pairs",
    )(
        neighbours.reshape(-1),
        counts.reshape(-1),
        domain_edge,
        coupling,
        sigma_table.reshape(1, types),
        depth_table.reshape(1, types),
        charge_table.reshape(1, types),
        *columns,
    )
    forces = forces.reshape(3, 1, 1, 1, atom_count)
    for axis in ("dz", "dy", "dx"):
        sums = summed(sums, axis)
    sums = sums * (0.5 / (atom_count * count_x * count_y * count_z))
    return (forces, sums[0, 0:1], sums[0, 1:2])


def solution(mesh):
    return jax.shard_map(
        on_device,
        mesh=mesh,
        in_specs=(
            P(None, ("win", "dx"), "dy", "dz", None),
            P(("win", "dx"), "dy", "dz", None),
            P(("win", "dx"), "dy", "dz", None),
            P(("win", "dx"), "dy", "dz", None, None),
            P(("win", "dx"), "dy", "dz", None, None),
            P(("win", "dx"), "dy", "dz", None),
            P(),
            P(),
            P(),
            P(),
            P("win"),
        ),
        out_specs=(P(None, ("win", "dx"), "dy", "dz", None), P("win"), P("win")),
        check_vma=False,
    )
```

time: 155 us -> 53.5 us (0.35)
  other arithmetic: 41.6 us -> 2.64 us
  blocking collectives: 31.8 us -> 0 us
  loops' own time: 20 us -> 0 us
  local copies, waits for them, and re-layouts: 23.9 us -> 7.05 us
  Pallas kernels: 0 us -> 13.8 us
  waiting for transfers between devices: 21.5 us -> 10.8 us
  starting transfers between devices: 10.9 us -> 17.5 us
  between operations: 4.44 us -> 1.33 us
    psum x1 -> x0, blocking collectives: 31.8 us -> none  [on_device(): lax.psum((jnp.sum(energies), jnp.sum(dhdls)), ('dx', 'dy', 'dz'))]
    reduce_sum x21 -> x0, other arithmetic: 30.2 us -> none  [the longest x6 23.1 us: pair_block(): jnp.sum(flagged * (-total_pair + weight * (grad_six * sigma_six * soft_al...]
    another operation x1 -> x0, loops' own time: 20 us -> none  [on_device(): lax.map(one_block, jnp.arange(block_total, dtype=jnp.int32))]
    pallas_call x0 -> x3, Pallas kernels: none -> 13.8 us  [the longest x1 10.6 us: on_device(): pl.pallas_call(functools.partial(pair_kernel, blocks, spacing, images), i...]
    ppermute x7 -> x10, waiting for transfers between devices: 21.5 us -> 10.8 us  [the longest x4 4.48 us: summed(): lax.ppermute(value, axis, [(i, i ^ step) for i in range(count)])]
    dynamic_update_slice x18 -> x0, local copies, waits for them, and re-layouts: 9.16 us -> none  [on_device(): lax.map(one_block, jnp.arange(block_total, dtype=jnp.int32))]
    dynamic_slice x18 -> x0, local copies, waits for them, and re-layouts: 7.08 us -> none  [the longest x6 3.52 us: one_block(): listed_count[block_id]]
    ppermute x7 -> x10, starting transfers between devices: 10.9 us -> 17.5 us  [the longest x4 9.57 us: summed(): lax.ppermute(value, axis, [(i, i ^ step) for i in range(count)])]
  transfers between devices with their start and end apart: 7 -> 10, of which waited for: 6 -> 8; matrix products, arithmetic and copies ran while one was open for 2% -> 5% of each run, Pallas kernels for 0% -> 0%
where the time goes in v1:
time: 53.5 us; the launch traced here: 53 us
  starting transfers between devices  17.5 us (33%)
  Pallas kernels  13.8 us (26%)
  waiting for transfers between devices  10.8 us (20%)
  local copies, waits for them, and re-layouts  7.05 us (13%)
  other arithmetic  2.64 us (5%)
  between operations  1.33 us (2%)
    pallas_call x1, Pallas kernels, on_device(): pl.pallas_call(functools.partial(pair_kernel, blocks, spacing, images), i...  10.6 us
    ppermute x4, starting transfers between devices, summed(): lax.ppermute(value, axis, [(i, i ^ step) for i in range(count)])  9.57 us
    ppermute x1, starting transfers between devices, on_device(): above = lax.ppermute(packed, 'dx', ring(count_x, 1))  5.08 us
    ppermute x4, waiting for transfers between devices, summed(): lax.ppermute(value, axis, [(i, i ^ step) for i in range(count)])  4.48 us
    ppermute x1, waiting for transfers between devices, on_device(): below2 = lax.ppermute(leavers, 'dx', ring(count_x, -2))  3.53 us
    unnamed x4, other arithmetic  2.63 us
    ppermute x3, waiting for transfers between devices, on_device(): lax.ppermute(moved, ('dy', 'dz'), grid_ring(count_y, count_z, *key))  2.19 us
    unnamed x18, local copies, waits for them, and re-layouts  1.93 us
  transfers between devices with their start and end apart: 10, of which 8 were waited for; matrix products, arithmetic and copies ran while one was open for 5% of the time, Pallas kernels for 0%

profile of v1, /device:TPU:0, one launch (start us, length us, event | category | flops | bytes accessed | tf_op | source)
XLA Modules:
  0.0 53.0 jit_solution(13245064751332636125)
XLA Ops:
  0.6 1.3 %reshape.44.leaving = s32[1,32]{1,0:T(1,128)} reshape(s32[1,1,1,2,16]{4,3,2,1,0:T(2,128)} %param.14) | data formatting | bytes 256 | tf_op jit(solution)/shard_map/reshape | solution.py:268
  1.9 1.3 %reduce.2 = s32[768]{0:T(1024)} reduce(s32[1,1,1,768]{3,2,1,0:T(1,128)} %param.12, s32[]{:T(128)} %constant.9), dimensions={0,1,2}, to_apply=%param.12.reduce_sub_computation | reduce | bytes 6148 | tf_op args[1]
  3.2 1.3 %reduce.3 = s32[768]{0:T(1024)} reduce(s32[1,1,1,768]{3,2,1,0:T(1,128)} %param.13, s32[]{:T(128)} %constant.9), dimensions={0,1,2}, to_apply=%param.13.reduce_sub_computation | reduce | bytes 6148 | tf_op args[2]
  4.5 0.6 %reshape.41.fraction = f32[18,128]{1,0:T(8,128)} reshape(f32[3,768]{1,0:T(4,128)S(1)} %reduce.1) | data formatting | bytes 18432 | tf_op jit(solution)/shard_map/reshape | solution.py:265
  5.1 1.4 %pack.1.own = f32[48,128]{1,0:T(8,128)} custom-call(f32[18,128]{1,0:T(8,128)} %reshape.41.fraction, s32[6,128]{1,0:T(8,128)} %bitcast.8, s32[6,128]{1,0:T(8,128)} %bitcast.9, s32[1,32]{1,0:T(1,128)} %reshape.44.leaving), custom_call_target="tpu_custom_call" | custom-call | tf_op jit(solution)/shard_map/pack/pallas_call | solution.py:257
  6.6 5.1 %collective-permute-start.2 = (f32[48,128]{1,0:T(8,128)}, f32[48,128]{1,0:T(8,128)S(1)}, u32[]{:S(2)}, u32[]{:S(2)}) collective-permute-start(f32[48,128]{1,0:T(8,128)} %pack.1.own), channel_id=1, source_target_pairs={{4,0},{8,4},{12,8},{0,12},{5,1},{9,5},{13,9},{1,13},{6,2},{10,6},{... | collective-permute-start | bytes 73736 | tf_op jit(solution)/shard_map/ppermute | solution.py:271
  11.6 0.8 %slice.12 = f32[8,128]{1,0:T(8,128)S(1)} slice(f32[48,128]{1,0:T(8,128)} %pack.1.own), slice={[40:48], [0:128]} | slice | bytes 8192 | tf_op jit(solution)/shard_map/slice | solution.py:272
  12.4 1.0 %collective-permute-start = (f32[8,128]{1,0:T(8,128)S(1)}, f32[8,128]{1,0:T(8,128)S(1)}, u32[]{:S(2)}, u32[]{:S(2)}) collective-permute-start(f32[8,128]{1,0:T(8,128)S(1)} %slice.12), channel_id=1, source_target_pairs={{8,0},{12,4},{0,8},{4,12},{9,1},{13,5},{1,9},{5,13},{10,2},{14,6},... | collective-permute-start | bytes 12296 | tf_op jit(solution)/shard_map/ppermute | solution.py:273
  13.4 3.5 %collective-permute-done.below2.above2 = f32[8,128]{1,0:T(8,128)S(1)} collective-permute-done((f32[8,128]{1,0:T(8,128)S(1)}, f32[8,128]{1,0:T(8,128)S(1)}, u32[]{:S(2)}, u32[]{:S(2)}) %collective-permute-start) | collective-permute-done | bytes 4128 | tf_op jit(solution)/shard_map/ppermute | solution.py:273
  17.5 0.6 %copy-done.4 = f32[48,128]{1,0:T(8,128)} copy-done((f32[48,128]{1,0:T(8,128)}, f32[48,128]{1,0:T(8,128)S(1)}, u32[]{:S(2)}) %copy-start.4) | copy-done | bytes 24600
  18.1 1.8 %migrate.1.refs_0_ = f32[96,128]{1,0:T(8,128)} custom-call(f32[8,128]{1,0:T(8,128)} %copy-done.5, f32[48,128]{1,0:T(8,128)} %copy-done.4, f32[48,128]{1,0:T(8,128)} %pack.1.own, f32[48,128]{1,0:T(8,128)} %copy-done.3, f32[8,128]{1,0:T(8,128)} %copy-done.5), custom_call_target="tpu_custom_call" | custom-call | tf_op jit(solution)/shard_map/migrate/pallas_call | solution.py:278
  19.9 1.5 %collective-permute-start.4 = (f32[96,128]{1,0:T(8,128)}, f32[96,128]{1,0:T(8,128)S(1)}, u32[]{:S(2)}, u32[]{:S(2)}) collective-permute-start(f32[96,128]{1,0:T(8,128)} %migrate.1.refs_0_), channel_id=1, source_target_pairs={{2,0},{3,1},{0,2},{1,3},{6,4},{7,5},{4,6},{5,7},{10,8},{11,9},{8,1... | collective-permute-start | bytes 147464 | tf_op jit(solution)/shard_map/ppermute | solution.py:292
  23.0 1.2 %collective-permute-done.4.refs_2_ = f32[96,128]{1,0:T(8,128)S(1)} collective-permute-done((f32[96,128]{1,0:T(8,128)}, f32[96,128]{1,0:T(8,128)S(1)}, u32[]{:S(2)}, u32[]{:S(2)}) %collective-permute-start.4) | collective-permute-done | bytes 49184 | tf_op jit(solution)/shard_map/ppermute | solution.py:292
  24.3 1.0 %collective-permute-done.3.refs_1_ = f32[96,128]{1,0:T(8,128)S(1)} collective-permute-done((f32[96,128]{1,0:T(8,128)}, f32[96,128]{1,0:T(8,128)S(1)}, u32[]{:S(2)}, u32[]{:S(2)}) %collective-permute-start.3) | collective-permute-done | bytes 49184 | tf_op jit(solution)/shard_map/ppermute | solution.py:292
  25.2 0.6 %copy-done.2 = f32[96,128]{1,0:T(8,128)} copy-done((f32[96,128]{1,0:T(8,128)}, f32[96,128]{1,0:T(8,128)S(1)}, u32[]{:S(2)}) %copy-start.2) | copy-done | bytes 49176
  25.8 10.6 %pairs.1 = (f32[18,128]{1,0:T(8,128)}, f32[1,128]{1,0:T(1,128)}) custom-call(s32[96]{0:T(128)} %reshape.36.listed, s32[6]{0:T(128)} %bitcast.10, f32[3]{0:T(128)} %edge.1, f32[1]{0:T(128)S(6)} %copy.16.coupling, f32[1,32]{1,0:T(1,128)} %bitcast.11, f32[1,32]{1,0:T(1,128)} %bitcast.12, f32[1,32]{1,0:T(1,128)} %bitcast.13, f32[96,128]{1,0:T(8,128)} %migrate.1.refs_0_, ...), custom_call_target="tpu_custom_call" | custom-call | tf_op jit(solution)/shard_map/pairs/pallas_call | solution.py:296
  36.4 0.7 %copy-done.8 = f32[1,128]{1,0:T(1,128)S(1)} copy-done((f32[1,128]{1,0:T(1,128)S(1)}, f32[1,128]{1,0:T(1,128)}, u32[]{:S(2)}) %copy-start.8) | copy-done | bytes 536
  37.1 1.2 %collective-permute-done.6 = f32[1,128]{1,0:T(1,128)S(1)} collective-permute-done((f32[1,128]{1,0:T(1,128)S(1)}, f32[1,128]{1,0:T(1,128)S(1)}, u32[]{:S(2)}, u32[]{:S(2)}) %collective-permute-start.6) | collective-permute-done | bytes 544 | tf_op jit(solution)/shard_map/ppermute | solution.py:230
  38.2 2.6 %collective-permute-start.7 = (f32[1,128]{1,0:T(1,128)S(1)}, f32[1,128]{1,0:T(1,128)S(1)}, u32[]{:S(2)}, u32[]{:S(2)}) collective-permute-start(f32[1,128]{1,0:T(1,128)S(1)} %add.12), channel_id=1, source_target_pairs={{0,2},{2,0},{1,3},{3,1},{4,6},{6,4},{5,7},{7,5},{8,10},{10,8},{9,1... | collective-permute-start | bytes 1544 | tf_op jit(solution)/shard_map/ppermute | solution.py:230
  40.8 1.5 %collective-permute-done.7 = f32[1,128]{1,0:T(1,128)S(1)} collective-permute-done((f32[1,128]{1,0:T(1,128)S(1)}, f32[1,128]{1,0:T(1,128)S(1)}, u32[]{:S(2)}, u32[]{:S(2)}) %collective-permute-start.7) | collective-permute-done | bytes 544 | tf_op jit(solution)/shard_map/ppermute | solution.py:230
  42.4 2.6 %collective-permute-start.8 = (f32[1,128]{1,0:T(1,128)S(1)}, f32[1,128]{1,0:T(1,128)S(1)}, u32[]{:S(2)}, u32[]{:S(2)}) collective-permute-start(f32[1,128]{1,0:T(1,128)S(1)} %add.13), channel_id=1, source_target_pairs={{0,4},{4,0},{8,12},{12,8},{1,5},{5,1},{9,13},{13,9},{2,6},{6,2},{1... | collective-permute-start | bytes 1544 | tf_op jit(solution)/shard_map/ppermute | solution.py:230
  45.0 1.5 %collective-permute-done.8 = f32[1,128]{1,0:T(1,128)S(1)} collective-permute-done((f32[1,128]{1,0:T(1,128)S(1)}, f32[1,128]{1,0:T(1,128)S(1)}, u32[]{:S(2)}, u32[]{:S(2)}) %collective-permute-start.8) | collective-permute-done | bytes 544 | tf_op jit(solution)/shard_map/ppermute | solution.py:230
  46.5 4.4 %collective-permute-start.9 = (f32[1,128]{1,0:T(1,128)S(1)}, f32[1,128]{1,0:T(1,128)S(1)}, u32[]{:S(2)}, u32[]{:S(2)}) collective-permute-start(f32[1,128]{1,0:T(1,128)S(1)} %add.14), channel_id=1, source_target_pairs={{0,8},{4,12},{8,0},{12,4},{1,9},{5,13},{9,1},{13,5},{2,10},{6,14},... | collective-permute-start | bytes 1544 | tf_op jit(solution)/shard_map/ppermute | solution.py:230
  50.9 1.3 %reshape.46 = f32[3,1,1,1,768]{4,3,2,1,0:T(1,128)} reshape(f32[18,128]{1,0:T(8,128)} %get-tuple-element.5) | data formatting | bytes 18432 | tf_op jit(solution)/shard_map/reshape | solution.py:323
  (31 shorter events, 2.5 us)
Async XLA Ops:
  0.6 3.9 %copy-start.6 = (f32[3,1,1,1,768]{4,3,2,1,0:T(1,128)S(1)}, f32[3,1,1,1,768]{4,3,2,1,0:T(1,128)}, u32[]{:S(2)}) copy-start(f32[3,1,1,1,768]{4,3,2,1,0:T(1,128)} %param.11) | copy-start | bytes 27652
  6.6 10.3 %collective-permute-start.2 = (f32[48,128]{1,0:T(8,128)}, f32[48,128]{1,0:T(8,128)S(1)}, u32[]{:S(2)}, u32[]{:S(2)}) collective-permute-start(f32[48,128]{1,0:T(8,128)} %pack.1.own), channel_id=1, source_target_pairs={{4,0},{8,4},{12,8},{0,12},{5,1},{9,5},{13,9},{1,13},{6,2},{10,6},{... | collective-permute-start | bytes 73736 | tf_op jit(solution)/shard_map/ppermute | solution.py:271
  11.6 5.8 %collective-permute-start.1 = (f32[48,128]{1,0:T(8,128)}, f32[48,128]{1,0:T(8,128)S(1)}, u32[]{:S(2)}, u32[]{:S(2)}) collective-permute-start(f32[48,128]{1,0:T(8,128)} %pack.1.own), channel_id=1, source_target_pairs={{12,0},{0,4},{4,8},{8,12},{13,1},{1,5},{5,9},{9,13},{14,2},{2,6},{... | collective-permute-start | bytes 73736 | tf_op jit(solution)/shard_map/ppermute | solution.py:270
  12.4 4.5 %collective-permute-start = (f32[8,128]{1,0:T(8,128)S(1)}, f32[8,128]{1,0:T(8,128)S(1)}, u32[]{:S(2)}, u32[]{:S(2)}) collective-permute-start(f32[8,128]{1,0:T(8,128)S(1)} %slice.12), channel_id=1, source_target_pairs={{8,0},{12,4},{0,8},{4,12},{9,1},{13,5},{1,9},{5,13},{10,2},{14,6},... | collective-permute-start | bytes 12296 | tf_op jit(solution)/shard_map/ppermute | solution.py:273
  16.9 0.6 %copy-start.5 = (f32[8,128]{1,0:T(8,128)}, f32[8,128]{1,0:T(8,128)S(1)}, u32[]{:S(2)}) copy-start(f32[8,128]{1,0:T(8,128)S(1)} %collective-permute-done.below2.above2) | copy-start | bytes 12292
  16.9 0.6 %copy-start.3 = (f32[48,128]{1,0:T(8,128)}, f32[48,128]{1,0:T(8,128)S(1)}, u32[]{:S(2)}) copy-start(f32[48,128]{1,0:T(8,128)S(1)} %collective-permute-done.2.above) | copy-start | bytes 73732
  17.5 0.6 %copy-start.4 = (f32[48,128]{1,0:T(8,128)}, f32[48,128]{1,0:T(8,128)S(1)}, u32[]{:S(2)}) copy-start(f32[48,128]{1,0:T(8,128)S(1)} %collective-permute-done.1.below) | copy-start | bytes 73732
  18.1 4.3 %copy-start.7 = (s32[1,1,1,6,16]{4,2,3,1,0:T(1,128)S(1)}, s32[1,1,1,6,16]{4,2,3,1,0:T(1,128)}, u32[]{:S(2)}) copy-start(s32[1,1,1,6,16]{4,2,3,1,0:T(1,128)} %param.15) | copy-start | bytes 1156
  19.9 3.1 %collective-permute-start.5 = (f32[96,128]{1,0:T(8,128)}, f32[96,128]{1,0:T(8,128)S(1)}, u32[]{:S(2)}, u32[]{:S(2)}) collective-permute-start(f32[96,128]{1,0:T(8,128)} %migrate.1.refs_0_), channel_id=1, source_target_pairs={{1,0},{0,1},{3,2},{2,3},{5,4},{4,5},{7,6},{6,7},{9,8},{8,9},{11,10... | collective-permute-start | bytes 147464 | tf_op jit(solution)/shard_map/ppermute | solution.py:292
  19.9 4.4 %collective-permute-start.4 = (f32[96,128]{1,0:T(8,128)}, f32[96,128]{1,0:T(8,128)S(1)}, u32[]{:S(2)}, u32[]{:S(2)}) collective-permute-start(f32[96,128]{1,0:T(8,128)} %migrate.1.refs_0_), channel_id=1, source_target_pairs={{2,0},{3,1},{0,2},{1,3},{6,4},{7,5},{4,6},{5,7},{10,8},{11,9},{8,1... | collective-permute-start | bytes 147464 | tf_op jit(solution)/shard_map/ppermute | solution.py:292
  21.4 3.8 %collective-permute-start.3 = (f32[96,128]{1,0:T(8,128)}, f32[96,128]{1,0:T(8,128)S(1)}, u32[]{:S(2)}, u32[]{:S(2)}) collective-permute-start(f32[96,128]{1,0:T(8,128)} %migrate.1.refs_0_), channel_id=1, source_target_pairs={{3,0},{2,1},{1,2},{0,3},{7,4},{6,5},{5,6},{4,7},{11,8},{10,9},{9,1... | collective-permute-start | bytes 147464 | tf_op jit(solution)/shard_map/ppermute | solution.py:292
  23.0 2.2 %copy-start = (f32[96,128]{1,0:T(8,128)}, f32[96,128]{1,0:T(8,128)S(1)}, u32[]{:S(2)}) copy-start(f32[96,128]{1,0:T(8,128)S(1)} %collective-permute-done.5.refs_3_) | copy-start | bytes 147460
  24.3 1.0 %copy-start.1 = (f32[96,128]{1,0:T(8,128)}, f32[96,128]{1,0:T(8,128)S(1)}, u32[]{:S(2)}) copy-start(f32[96,128]{1,0:T(8,128)S(1)} %collective-permute-done.4.refs_2_) | copy-start | bytes 147460
  25.2 0.6 %copy-start.2 = (f32[96,128]{1,0:T(8,128)}, f32[96,128]{1,0:T(8,128)S(1)}, u32[]{:S(2)}) copy-start(f32[96,128]{1,0:T(8,128)S(1)} %collective-permute-done.3.refs_1_) | copy-start | bytes 147460
  36.4 0.7 %copy-start.8 = (f32[1,128]{1,0:T(1,128)S(1)}, f32[1,128]{1,0:T(1,128)}, u32[]{:S(2)}) copy-start(f32[1,128]{1,0:T(1,128)} %get-tuple-element.6) | copy-start | bytes 1540
  37.1 1.2 %collective-permute-start.6 = (f32[1,128]{1,0:T(1,128)S(1)}, f32[1,128]{1,0:T(1,128)S(1)}, u32[]{:S(2)}, u32[]{:S(2)}) collective-permute-start(f32[1,128]{1,0:T(1,128)S(1)} %copy-done.8), channel_id=1, source_target_pairs={{0,1},{1,0},{2,3},{3,2},{4,5},{5,4},{6,7},{7,6},{8,9},{9,8},{10,11... | collective-permute-start | bytes 1544 | tf_op jit(solution)/shard_map/ppermute | solution.py:230
  38.2 4.1 %collective-permute-start.7 = (f32[1,128]{1,0:T(1,128)S(1)}, f32[1,128]{1,0:T(1,128)S(1)}, u32[]{:S(2)}, u32[]{:S(2)}) collective-permute-start(f32[1,128]{1,0:T(1,128)S(1)} %add.12), channel_id=1, source_target_pairs={{0,2},{2,0},{1,3},{3,1},{4,6},{6,4},{5,7},{7,5},{8,10},{10,8},{9,1... | collective-permute-start | bytes 1544 | tf_op jit(solution)/shard_map/ppermute | solution.py:230
  42.4 4.1 %collective-permute-start.8 = (f32[1,128]{1,0:T(1,128)S(1)}, f32[1,128]{1,0:T(1,128)S(1)}, u32[]{:S(2)}, u32[]{:S(2)}) collective-permute-start(f32[1,128]{1,0:T(1,128)S(1)} %add.13), channel_id=1, source_target_pairs={{0,4},{4,0},{8,12},{12,8},{1,5},{5,1},{9,13},{13,9},{2,6},{6,2},{1... | collective-permute-start | bytes 1544 | tf_op jit(solution)/shard_map/ppermute | solution.py:230
  46.5 5.9 %collective-permute-start.9 = (f32[1,128]{1,0:T(1,128)S(1)}, f32[1,128]{1,0:T(1,128)S(1)}, u32[]{:S(2)}, u32[]{:S(2)}) collective-permute-start(f32[1,128]{1,0:T(1,128)S(1)} %add.14), channel_id=1, source_target_pairs={{0,8},{4,12},{8,0},{12,4},{1,9},{5,13},{9,1},{13,5},{2,10},{6,14},... | collective-permute-start | bytes 1544 | tf_op jit(solution)/shard_map/ppermute | solution.py:230

commit v2 on v1

v2 whole, which is shorter than its diff:
```python
import functools

import jax
import jax.numpy as jnp
from jax import lax
from jax.experimental import pallas as pl
from jax.experimental.pallas import tpu as pltpu
from jax.sharding import PartitionSpec as P

soft_base = 0.3
soft_alpha = 0.5
charge_base = 0.3
charge_alpha = 0.5
coulomb = 0.1
LANES = 128
SUB = 8


def ring(count, by):
    return [((i + by) % count, i) for i in range(count)]


def grid_ring(count_y, count_z, by_y, by_z):
    route = []
    for y in range(count_y):
        for z in range(count_z):
            source = ((y + by_y) % count_y) * count_z + (z + by_z) % count_z
            route.append((source, y * count_z + z))
    return route


def near(array):
    return pltpu.with_memory_space_constraint(array, pltpu.VMEM)


def gather_lanes(rows, lanes):
    return jnp.take_along_axis(rows, lanes, axis=1, mode="promise_in_bounds")


def pack_kernel(
    blocks, fraction, kind, flag, leaving, sigma_t, depth_t, charge_t, out, leavers, tables
):
    tables[...] = jnp.zeros(tables.shape, jnp.float32)
    type_rows(tables, sigma_t, depth_t, charge_t)
    mig = leaving.shape[-1]
    head = out.shape[0] - 2 * SUB
    out[5 * blocks :, :] = jnp.zeros((out.shape[0] - 5 * blocks, LANES), jnp.float32)
    for q in range(blocks):
        part = slice(q * LANES, q * LANES + LANES)
        for k in range(3):
            out[k * blocks + q : k * blocks + q + 1, :] = fraction[k, 0, 0, :, part]
        at = 3 * blocks + q
        out[at : at + 1, :] = kind[0, 0, :, part].astype(jnp.float32)
        at = 4 * blocks + q
        out[at : at + 1, :] = flag[0, 0, :, part].astype(jnp.float32)
    for side in range(2):
        out[head : head + 1, side * mig : side * mig + mig] = leaving[
            0, 0, 0, side : side + 1, :
        ].astype(jnp.float32)
    slots = jnp.broadcast_to(out[head : head + 1, :], (SUB, LANES)).astype(jnp.int32)
    lane = slots & (LANES - 1)
    here = lax.broadcasted_iota(jnp.int32, (SUB, LANES), 0) == (slots >> 7)
    for k in range(5):
        picked = gather_lanes(out[k * blocks : k * blocks + SUB, :], lane)
        picked = jnp.sum(jnp.where(here, picked, 0.0), axis=0, keepdims=True)
        at = head + SUB + k
        out[at : at + 1, :] = picked
    leavers[...] = out[head + SUB :, :]


def migrate_kernel(blocks, mig, below2, below, own, above, above2, out):
    pad = own.shape[0] - 2 * SUB
    tail = pad + SUB
    leavers = [
        below2[...],
        below[tail : tail + SUB, :],
        own[tail : tail + SUB, :],
        above[tail : tail + SUB, :],
        above2[...],
    ]
    lane = lax.broadcasted_iota(jnp.int32, (SUB, LANES), 1)
    row = lax.broadcasted_iota(jnp.int32, (SUB, LANES), 0)
    place = row * LANES + lane
    shift = jnp.where(row == 0, 1.0, 0.0)
    for d, base in enumerate((below, own, above)):
        slots = jnp.broadcast_to(base[pad : pad + 1, :], (SUB, LANES)).astype(jnp.int32)
        from_above = pltpu.roll(leavers[d + 2], LANES - mig, 1) + shift
        from_below = pltpu.roll(leavers[d], mig, 1) - shift
        incoming = jnp.where(lane < mig, from_above, from_below)
        origin = jnp.full((SUB, LANES), -1, jnp.int32)
        for m in range(2 * mig):
            spot = jnp.broadcast_to(slots[:, m : m + 1], (SUB, LANES))
            origin = jnp.where(place == spot, m, origin)
        arrives = origin >= 0
        source = jnp.maximum(origin, 0)
        for k in range(5):
            fresh = gather_lanes(jnp.broadcast_to(incoming[k : k + 1, :], (SUB, LANES)), source)
            held = base[k * blocks : k * blocks + SUB, :]
            kept = jnp.where(arrives, fresh, held)
            start = d * pad + k * blocks
            out[start : start + blocks, :] = kept[0:blocks]


def type_rows(tables, sigma_t, depth_t, charge_t):
    types = sigma_t.shape[1]
    tables[0, :, 0:types] = jnp.broadcast_to(0.5 * sigma_t[...], (SUB, types))
    tables[1, :, 0:types] = jnp.broadcast_to(2.0 * jnp.sqrt(depth_t[...]), (SUB, types))
    tables[2, :, 0:types] = jnp.broadcast_to(charge_t[...], (SUB, types))


def domain_rows(column, a, blocks, tables):
    pad = column.shape[0] // 3
    part = [column[a * pad + k * blocks : a * pad + k * blocks + SUB, :] for k in range(5)]
    kind = part[3].astype(jnp.int32)
    return part[0:3], [gather_lanes(tables[t], kind) for t in range(3)] + [part[4]]


def positions(spots, steps, edge, spacing):
    return [
        (spot + float(step - 1)) * edge[dim] * spacing
        for dim, (spot, step) in enumerate(zip(spots, steps))
    ]


def spread_kernel(
    blocks, spacing, edge, coupling, tables, moved, own, selves, staged
):
    lam = coupling[0]
    spots, fixed = domain_rows(moved, 1, blocks, tables)
    rows = positions(spots, (1, 1, 1), edge, spacing) + fixed
    staged[...] = jnp.zeros(staged.shape, jnp.float32)
    for k in range(7):
        staged[SUB * k : SUB * k + blocks, :] = rows[k][0:blocks]
    flag, eps, charge = rows[6], rows[4], rows[5]
    a = soft_base + soft_alpha * (lam * flag)
    u = 1.0 / a
    t = eps * eps * u
    tu = t * u
    lj = tu - t
    rs = lax.rsqrt(a)
    vc = coulomb * charge * charge * rs
    v = lj + vc
    real = lax.broadcasted_iota(jnp.int32, (SUB, LANES), 0) < blocks
    selves[0] = jnp.where(real, v, 0.0)
    selves[1] = jnp.where(real, flag * v, 0.0)
    selves[2] = jnp.where(real, flag * ((lj + tu) * u + 0.5 * (vc * (rs * rs))), 0.0)
    columns_of = staged[...].T
    for q in range(blocks):
        for k in range(7):
            lane = SUB * k + q
            spread = jnp.broadcast_to(columns_of[:, lane : lane + 1], (LANES, LANES))
            if k == 5:
                spread = spread * coulomb
            own[q, k] = spread
            if k == 6:
                own[q, 7] = soft_base + soft_alpha * (lam * spread)
                own[q, 8] = 1.0 - lam * spread


def pair_kernel(
    blocks, spacing, images, listed, counts, edge, coupling, tables, own, selves, *refs
):
    columns = refs[: max(c for c, _ in images) + 1]
    acc, sums = refs[len(columns) : len(columns) + 2]
    (ghost,) = refs[len(columns) + 2 :]
    lam = coupling[0]
    for column in range(len(columns)):
        for a in range(3):
            spots, fixed = domain_rows(columns[column], a, blocks, tables)
            for where, (b, c) in images:
                if where != column:
                    continue
                at = (9 * a + 3 * b + c) * blocks
                rows = positions(spots, (a, b, c), edge, spacing) + fixed
                for k in range(7):
                    ghost[k, at : at + blocks, :] = rows[k][0:blocks]
    centre = 13 * blocks
    row = lax.broadcasted_iota(jnp.int32, (SUB, LANES), 0)
    slots = listed.shape[0] // blocks

    def block(q, totals):
        acc[q] = jnp.zeros(acc.shape[1:], jnp.float32)

        def entry(e, carry):
            sum_v, sum_pv, sum_pg, itself = carry
            h = listed[q * slots + e]
            other = [
                jnp.broadcast_to(ghost[k, pl.ds(h, 1), :], (SUB, LANES)) for k in range(7)
            ]
            other_a = soft_base + soft_alpha * (lam * other[6])
            other_w = 1.0 - lam * other[6]
            for g in range(LANES // SUB):
                at = slice(g * SUB, g * SUB + SUB)
                dx = own[q, 0, at, :] - other[0]
                dy = own[q, 1, at, :] - other[1]
                dz = own[q, 2, at, :] - other[2]
                r2 = dx * dx + dy * dy + dz * dz
                sigma = own[q, 3, at, :] + other[3]
                eps4 = own[q, 4, at, :] * other[4]
                qq = own[q, 5, at, :] * other[5]
                p = jnp.maximum(own[q, 6, at, :], other[6])
                a = jnp.maximum(own[q, 7, at, :], other_a)
                w = jnp.minimum(own[q, 8, at, :], other_w)
                s2 = sigma * sigma
                s6 = s2 * s2 * s2
                r4 = r2 * r2
                root = lax.rsqrt(s6 * a + r4 * r2)
                inv = root * root
                rs = lax.rsqrt(a + r2)
                u = s6 * inv
                t = eps4 * u
                tu = t * u
                lj = tu - t
                k = lj + tu
                vc = qq * rs
                vcr = vc * (rs * rs)
                f = w * (vcr + 6.0 * (k * (r4 * inv)))
                acc[q, 0, at, :] += f * dx
                acc[q, 1, at, :] += f * dy
                acc[q, 2, at, :] += f * dz
                v = lj + vc
                sum_v = sum_v + v
                sum_pv = sum_pv + p * v
                sum_pg = sum_pg + p * (k * u + 0.5 * vcr)
            return sum_v, sum_pv, sum_pg, itself + jnp.where(h == centre + q, 1.0, 0.0)

        *sums_of, itself = lax.fori_loop(0, counts[q], entry, totals + (jnp.float32(0.0),))
        held = jnp.where(row == q, itself, 0.0)
        return tuple(total - held * selves[k] for k, total in enumerate(sums_of))

    zero = jnp.zeros((SUB, LANES), jnp.float32)
    sum_v, sum_pv, sum_pg = lax.fori_loop(0, blocks, block, (zero, zero, zero))
    energy = sum_v - lam * sum_pv
    dhdl = -sum_pv - 0.5 * (1.0 - lam) * sum_pg
    energy = jnp.sum(jnp.sum(energy, axis=0, keepdims=True), axis=1, keepdims=True)
    dhdl = jnp.sum(jnp.sum(dhdl, axis=0, keepdims=True), axis=1, keepdims=True)
    lane = lax.broadcasted_iota(jnp.int32, (1, LANES), 1)
    sums[...] = jnp.where(lane == 0, energy, jnp.where(lane == 1, dhdl, 0.0))


def finish_kernel(blocks, acc, forces, turned):
    lane = lax.broadcasted_iota(jnp.int32, (LANES, LANES), 1)
    held = jnp.zeros((LANES, LANES), jnp.float32)
    for q in range(blocks):
        for k in range(3):
            total = jnp.sum(acc[q, k], axis=1, keepdims=True)
            held = jnp.where(lane == k * blocks + q, total, held)
    turned[...] = held.T
    for k in range(3):
        for q in range(blocks):
            at = k * blocks + q
            forces[k, 0, 0, :, q * LANES : q * LANES + LANES] = turned[at : at + 1, :]


def summed(value, axis):
    count = lax.axis_size(axis)
    if count & (count - 1):
        return lax.psum(value, axis)
    step = 1
    while step < count:
        value = value + lax.ppermute(value, axis, [(i, i ^ step) for i in range(count)])
        step *= 2
    return value


def on_device(
    fraction,
    atom_type,
    perturbed,
    leaving,
    neighbours,
    counts,
    sigma_table,
    depth_table,
    charge_table,
    domain_edge,
    coupling,
):
    atom_count = fraction.shape[-1]
    blocks = atom_count // LANES
    spacing = float(atom_count) ** (1.0 / 3.0)
    mig = leaving.shape[-1]
    types = sigma_table.shape[0]
    count_x, count_y, count_z = (lax.axis_size(axis) for axis in ("dx", "dy", "dz"))
    pad = -(-(5 * blocks) // SUB) * SUB
    vmem = pl.BlockSpec(memory_space=pltpu.VMEM)
    smem = pl.BlockSpec(memory_space=pltpu.SMEM)
    packed, leavers, tables = pl.pallas_call(
        functools.partial(pack_kernel, blocks),
        in_specs=[vmem] * 7,
        out_specs=[vmem] * 3,
        out_shape=[
            pltpu.VMEM((pad + 2 * SUB, LANES), jnp.float32),
            pltpu.VMEM((SUB, LANES), jnp.float32),
            pltpu.VMEM((3, SUB, LANES), jnp.float32),
        ],
        name="pack",
    )(
        fraction,
        atom_type,
        perturbed,
        leaving,
        *(table.reshape(1, types) for table in (sigma_table, depth_table, charge_table)),
    )
    below = lax.ppermute(packed, "dx", ring(count_x, -1))
    above = lax.ppermute(packed, "dx", ring(count_x, 1))
    below2 = lax.ppermute(leavers, "dx", ring(count_x, -2))
    if (count_x - 2) % count_x == 2 % count_x:
        above2 = below2
    else:
        above2 = lax.ppermute(leavers, "dx", ring(count_x, 2))
    moved = pl.pallas_call(
        functools.partial(migrate_kernel, blocks, mig),
        in_specs=[vmem] * 5,
        out_specs=vmem,
        out_shape=pltpu.VMEM((3 * pad, LANES), jnp.float32),
        name="migrate",
    )(*(near(part) for part in (below2, below, packed, above, above2)))
    places, columns, images = {(0, 0): 0}, [moved], []
    for b in range(3):
        for c in range(3):
            key = ((b - 1) % count_y, (c - 1) % count_z)
            if key not in places:
                places[key] = len(columns)
                columns.append(
                    lax.ppermute(moved, ("dy", "dz"), grid_ring(count_y, count_z, *key))
                )
            images.append((places[key], (b, c)))
    rows = -(-27 * blocks // SUB) * SUB
    own, selves = pl.pallas_call(
        functools.partial(spread_kernel, blocks, spacing),
        in_specs=[smem] * 2 + [vmem] * 2,
        out_specs=[vmem, vmem],
        out_shape=[
            pltpu.VMEM((blocks, 9, LANES, LANES), jnp.float32),
            pltpu.VMEM((3, SUB, LANES), jnp.float32),
        ],
        scratch_shapes=[pltpu.VMEM((LANES, LANES), jnp.float32)],
        cost_estimate=pl.CostEstimate(flops=4000000, bytes_accessed=0, transcendentals=0),
        compiler_params=pltpu.CompilerParams(vmem_limit_bytes=8 << 20),
        name="spread",
    )(domain_edge, coupling, near(tables), near(moved))
    acc, sums = pl.pallas_call(
        functools.partial(pair_kernel, blocks, spacing, images),
        in_specs=[smem] * 4 + [vmem] * (3 + len(columns)),
        out_specs=[vmem, vmem],
        out_shape=[
            pltpu.VMEM((blocks, 3, LANES, LANES), jnp.float32),
            pltpu.VMEM((1, LANES), jnp.float32),
        ],
        scratch_shapes=[
            pltpu.VMEM((7, rows, LANES), jnp.float32),
        ],
        compiler_params=pltpu.CompilerParams(vmem_limit_bytes=8 << 20),
        name="pairs",
    )(
        neighbours.reshape(-1),
        counts.reshape(-1),
        domain_edge,
        coupling,
        near(tables),
        near(own),
        near(selves),
        *(near(part) for part in columns),
    )
    forces = pl.pallas_call(
        functools.partial(finish_kernel, blocks),
        in_specs=[vmem],
        out_specs=vmem,
        out_shape=jax.ShapeDtypeStruct(fraction.shape, jnp.float32),
        scratch_shapes=[pltpu.VMEM((LANES, LANES), jnp.float32)],
        cost_estimate=pl.CostEstimate(flops=4000000, bytes_accessed=0, transcendentals=0),
        compiler_params=pltpu.CompilerParams(vmem_limit_bytes=8 << 20),
        name="finish",
    )(near(acc))
    for axis in ("dz", "dy", "dx"):
        sums = summed(sums, axis)
    sums = sums * (0.5 / (atom_count * count_x * count_y * count_z))
    return (forces, sums[0, 0:1], sums[0, 1:2])


def solution(mesh):
    return jax.shard_map(
        on_device,
        mesh=mesh,
        in_specs=(
            P(None, ("win", "dx"), "dy", "dz", None),
            P(("win", "dx"), "dy", "dz", None),
            P(("win", "dx"), "dy", "dz", None),
            P(("win", "dx"), "dy", "dz", None, None),
            P(("win", "dx"), "dy", "dz", None, None),
            P(("win", "dx"), "dy", "dz", None),
            P(),
            P(),
            P(),
            P(),
            P("win"),
        ),
        out_specs=(P(None, ("win", "dx"), "dy", "dz", None), P("win"), P("win")),
        check_vma=False,
    )
```

time: 53.5 us -> 41.1 us (0.77)
  local copies, waits for them, and re-layouts: 7.05 us -> 1.97 us
  Pallas kernels: 13.8 us -> 10.1 us
  starting transfers between devices: 17.5 us -> 14.8 us
  other arithmetic: 2.64 us -> 0.71 us
  waiting for transfers between devices: 10.8 us -> 12.2 us
    pallas_call x1, Pallas kernels: 10.6 us -> 6.23 us  [on_device(): pl.pallas_call(functools.partial(pair_kernel, blocks, spacing, images), i...]
    reshape x3 -> x0, local copies, waits for them, and re-layouts: 3.2 us -> none  [the longest x1 1.32 us: on_device(): forces = forces.reshape(3, 1, 1, 1, atom_count)]
    ppermute x4, waiting for transfers between devices: 4.48 us -> 7.59 us  [summed(): lax.ppermute(value, axis, [(i, i ^ step) for i in range(count)])]
    ppermute x4, starting transfers between devices: 9.57 us -> 6.76 us  [summed(): lax.ppermute(value, axis, [(i, i ^ step) for i in range(count)])]
    ppermute x3, waiting for transfers between devices: 2.19 us -> 0.01 us  [on_device(): lax.ppermute(moved, ('dy', 'dz'), grid_ring(count_y, count_z, *key))]
    pallas_call x1 -> x3, Pallas kernels: 1.43 us -> 3.45 us  [the longest x1 1.51 us: on_device(): pl.pallas_call(functools.partial(spread_kernel, blocks, spacing), in_spec...]
    unnamed x4 -> x1, other arithmetic: 2.63 us -> 0.7 us
    pallas_call x1, Pallas kernels: 1.77 us -> 0.43 us  [on_device(): pl.pallas_call(functools.partial(migrate_kernel, blocks, mig), in_specs=[...]
  transfers between devices with their start and end apart: 10 -> 10, of which waited for: 8 -> 6; matrix products, arithmetic and copies ran while one was open for 5% -> 2% of each run, Pallas kernels for 0% -> 6%
where the time goes in v2:
time: 41.1 us
  starting transfers between devices  14.8 us (36%)
  waiting for transfers between devices  12.2 us (30%)
  Pallas kernels  10.1 us (25%)
  local copies, waits for them, and re-layouts  1.97 us (5%)
  between operations  1.35 us (3%)
  other arithmetic  0.71 us (2%)
    ppermute x4, waiting for transfers between devices, summed(): lax.ppermute(value, axis, [(i, i ^ step) for i in range(count)])  7.59 us
    ppermute x4, starting transfers between devices, summed(): lax.ppermute(value, axis, [(i, i ^ step) for i in range(count)])  6.76 us
    pallas_call x1, Pallas kernels, on_device(): pl.pallas_call(functools.partial(pair_kernel, blocks, spacing, images), i...  6.23 us
    ppermute x1, starting transfers between devices, on_device(): above = lax.ppermute(packed, 'dx', ring(count_x, 1))  5.13 us
    ppermute x1, waiting for transfers between devices, on_device(): below2 = lax.ppermute(leavers, 'dx', ring(count_x, -2))  3.5 us
    ppermute x3, starting transfers between devices, on_device(): lax.ppermute(moved, ('dy', 'dz'), grid_ring(count_y, count_z, *key))  1.86 us
    pallas_call x1, Pallas kernels, on_device(): pl.pallas_call(functools.partial(spread_kernel, blocks, spacing), in_spec...  1.51 us
    unnamed x4, local copies, waits for them, and re-layouts  1.31 us
  transfers between devices with their start and end apart: 10, of which 6 were waited for; matrix products, arithmetic and copies ran while one was open for 2% of the time, Pallas kernels for 6%

profile of v2, /device:TPU:0, one launch (start us, length us, event | category | flops | bytes accessed | tf_op | source)
XLA Modules:
  0.0 41.1 jit_solution(18179307007049514382)
XLA Ops:
  0.6 0.9 %pack.1 = (f32[48,128]{1,0:T(8,128)S(1)}, f32[8,128]{1,0:T(8,128)S(1)}, f32[3,8,128]{2,1,0:T(8,128)S(1)}) custom-call(f32[3,1,1,1,768]{4,3,2,1,0:T(1,128)} %fraction.1, s32[1,1,1,768]{3,2,1,0:T(1,128)} %kind.1, s32[1,1,1,768]{3,2,1,0:T(1,128)} %flag.1, s32[1,1,1,2,16]{4,3,2,1,0:T(2,128)} %leaving.1, f32[1,32]{1,0:T(1,128)} %bitcast.7, f32[1,32]{1,0:T(1,128)} %bitcast.8, ...), custom_call_target="tpu_custom_call" | custom-call | tf_op jit(solution)/shard_map/pack/pallas_call | solution.py:288
  1.6 5.1 %collective-permute-start.2 = (f32[48,128]{1,0:T(8,128)S(1)}, f32[48,128]{1,0:T(8,128)S(1)}, u32[]{:S(2)}, u32[]{:S(2)}) collective-permute-start(f32[48,128]{1,0:T(8,128)S(1)} %get-tuple-element.12.own), channel_id=1, source_target_pairs={{4,0},{8,4},{12,8},{0,12},{5,1},{9,5},{13,9},{1,13},{6,2},{10,6},{... | collective-permute-start | bytes 73736 | tf_op jit(solution)/shard_map/ppermute | solution.py:306
  6.7 1.0 %collective-permute-start = (f32[8,128]{1,0:T(8,128)S(1)}, f32[8,128]{1,0:T(8,128)S(1)}, u32[]{:S(2)}, u32[]{:S(2)}) collective-permute-start(f32[8,128]{1,0:T(8,128)S(1)} %get-tuple-element.11), channel_id=1, source_target_pairs={{8,0},{12,4},{0,8},{4,12},{9,1},{13,5},{1,9},{5,13},{10,2},{14,6},... | collective-permute-start | bytes 12296 | tf_op jit(solution)/shard_map/ppermute | solution.py:307
  7.7 3.5 %collective-permute-done.below2.above2 = f32[8,128]{1,0:T(8,128)S(1)} collective-permute-done((f32[8,128]{1,0:T(8,128)S(1)}, f32[8,128]{1,0:T(8,128)S(1)}, u32[]{:S(2)}, u32[]{:S(2)}) %collective-permute-start) | collective-permute-done | bytes 4128 | tf_op jit(solution)/shard_map/ppermute | solution.py:307
  11.2 1.1 %collective-permute-done.1.below = f32[48,128]{1,0:T(8,128)S(1)} collective-permute-done((f32[48,128]{1,0:T(8,128)S(1)}, f32[48,128]{1,0:T(8,128)S(1)}, u32[]{:S(2)}, u32[]{:S(2)}) %collective-permute-start.1) | collective-permute-done | bytes 24608 | tf_op jit(solution)/shard_map/ppermute | solution.py:305
  12.3 0.4 %migrate.1.moved.refs_0_ = f32[96,128]{1,0:T(8,128)S(1)} custom-call(f32[8,128]{1,0:T(8,128)S(1)} %collective-permute-done.below2.above2, f32[48,128]{1,0:T(8,128)S(1)} %collective-permute-done.1.below, f32[48,128]{1,0:T(8,128)S(1)} %get-tuple-element.12.own, f32[48,128]{1,0:T(8,128)S(1)} %collective-permute-done.2.above, ...), custom_call_target="tpu_custom_call" | custom-call | tf_op jit(solution)/shard_map/migrate/pallas_call | solution.py:312
  12.7 0.0 collective-permute-start.5
  12.8 1.6 %collective-permute-start.4 = (f32[96,128]{1,0:T(8,128)S(1)}, f32[96,128]{1,0:T(8,128)S(1)}, u32[]{:S(2)}, u32[]{:S(2)}) collective-permute-start(f32[96,128]{1,0:T(8,128)S(1)} %migrate.1.moved.refs_0_), channel_id=1, source_target_pairs={{2,0},{3,1},{0,2},{1,3},{6,4},{7,5},{4,6},{5,7},{10,8},{11,9},{8,1... | collective-permute-start | bytes 147464 | tf_op jit(solution)/shard_map/ppermute | solution.py:326
  14.3 0.3 collective-permute-start.3
  15.3 0.7 %reduce = s32[6,16]{1,0:T(8,128)S(1)} reduce(s32[1,1,1,6,16]{4,2,3,1,0:T(1,128)} %param.15, s32[]{:T(128)} %constant.9), dimensions={0,1,2}, to_apply=%param.15.reduce_sub_computation | reduce | bytes 772 | tf_op args[4]
  16.0 0.1 reshape.21.listed
  16.0 0.7 %copy-done = f32[3]{0:T(128)S(1)} copy-done((f32[3]{0:T(128)S(1)}, f32[3]{0:T(128)}, u32[]{:S(2)}) %copy-start) | copy-done | bytes 36
  16.7 1.5 %spread.1 = (f32[6,9,128,128]{3,2,1,0:T(8,128)S(1)}, f32[3,8,128]{2,1,0:T(8,128)S(1)}) custom-call(f32[3]{0:T(128)S(1)} %copy-done, f32[1]{0:T(128)S(6)} %copy.14.coupling, f32[3,8,128]{2,1,0:T(8,128)S(1)} %get-tuple-element.10.tables, f32[96,128]{1,0:T(8,128)S(1)} %migrate.1.moved.refs_0_), custom_call_target="tpu_custom_call" | custom-call | flops 4000000 | tf_op jit(solution)/shard_map/spread/pallas_call | solution.py:330
  18.3 0.6 %copy-done.1 = s32[1,1,1,6]{3,2,1,0:T(1,128)S(1)} copy-done((s32[1,1,1,6]{3,2,1,0:T(1,128)S(1)}, s32[1,1,1,6]{3,2,1,0:T(1,128)}, u32[]{:S(2)}) %copy-start.1) | copy-done | bytes 48
  18.9 6.2 %pairs.1 = (f32[6,3,128,128]{3,2,1,0:T(8,128)S(1)}, f32[1,128]{1,0:T(1,128)S(1)}) custom-call(s32[96]{0:T(128)S(1)} %reshape.21.listed, s32[6]{0:T(128)S(1)} %bitcast.6, f32[3]{0:T(128)S(1)} %copy-done, f32[1]{0:T(128)S(6)} %copy.14.coupling, f32[3,8,128]{2,1,0:T(8,128)S(1)} %get-tuple-element.10.tables, f32[6,9,128,128]{3,2,1,0:T(8,128)S(1)} %get-tuple-element.13.own, ...), custom_call_target="tpu_custom_call" | custom-call | tf_op jit(solution)/shard_map/pairs/pallas_call | solution.py:343
  25.1 1.0 %collective-permute-start.6 = (f32[1,128]{1,0:T(1,128)S(1)}, f32[1,128]{1,0:T(1,128)S(1)}, u32[]{:S(2)}, u32[]{:S(2)}) collective-permute-start(f32[1,128]{1,0:T(1,128)S(1)} %get-tuple-element.16), channel_id=1, source_target_pairs={{0,1},{1,0},{2,3},{3,2},{4,5},{5,4},{6,7},{7,6},{8,9},{9,8},{10,11... | collective-permute-start | bytes 1544 | tf_op jit(solution)/shard_map/ppermute | solution.py:261
  26.1 0.8 %collective-permute-done.6 = f32[1,128]{1,0:T(1,128)S(1)} collective-permute-done((f32[1,128]{1,0:T(1,128)S(1)}, f32[1,128]{1,0:T(1,128)S(1)}, u32[]{:S(2)}, u32[]{:S(2)}) %collective-permute-start.6) | collective-permute-done | bytes 544 | tf_op jit(solution)/shard_map/ppermute | solution.py:261
  27.0 4.0 %collective-permute-start.7 = (f32[1,128]{1,0:T(1,128)S(1)}, f32[1,128]{1,0:T(1,128)S(1)}, u32[]{:S(2)}, u32[]{:S(2)}) collective-permute-start(f32[1,128]{1,0:T(1,128)S(1)} %add.12), channel_id=1, source_target_pairs={{0,2},{2,0},{1,3},{3,1},{4,6},{6,4},{5,7},{7,5},{8,10},{10,8},{9,1... | collective-permute-start | bytes 1544 | tf_op jit(solution)/shard_map/ppermute | solution.py:261
  30.9 1.5 %collective-permute-done.7 = f32[1,128]{1,0:T(1,128)S(1)} collective-permute-done((f32[1,128]{1,0:T(1,128)S(1)}, f32[1,128]{1,0:T(1,128)S(1)}, u32[]{:S(2)}, u32[]{:S(2)}) %collective-permute-start.7) | collective-permute-done | bytes 544 | tf_op jit(solution)/shard_map/ppermute | solution.py:261
  32.5 3.6 %collective-permute-done.8 = f32[1,128]{1,0:T(1,128)S(1)} collective-permute-done((f32[1,128]{1,0:T(1,128)S(1)}, f32[1,128]{1,0:T(1,128)S(1)}, u32[]{:S(2)}, u32[]{:S(2)}) %collective-permute-start.8) | collective-permute-done | bytes 544 | tf_op jit(solution)/shard_map/ppermute | solution.py:261
  36.1 1.8 %collective-permute-start.9 = (f32[1,128]{1,0:T(1,128)S(1)}, f32[1,128]{1,0:T(1,128)S(1)}, u32[]{:S(2)}, u32[]{:S(2)}) collective-permute-start(f32[1,128]{1,0:T(1,128)S(1)} %add.14), channel_id=1, source_target_pairs={{0,8},{4,12},{8,0},{12,4},{1,9},{5,13},{9,1},{13,5},{2,10},{6,14},... | collective-permute-start | bytes 1544 | tf_op jit(solution)/shard_map/ppermute | solution.py:261
  37.8 1.0 %finish.1 = f32[3,1,1,1,768]{4,3,2,1,0:T(1,128)} custom-call(f32[6,3,128,128]{3,2,1,0:T(8,128)S(1)} %get-tuple-element.15.acc), custom_call_target="tpu_custom_call" | custom-call | flops 4000000 | tf_op jit(solution)/shard_map/finish/pallas_call | solution.py:366
  38.9 1.7 %collective-permute-done.9 = f32[1,128]{1,0:T(1,128)S(1)} collective-permute-done((f32[1,128]{1,0:T(1,128)S(1)}, f32[1,128]{1,0:T(1,128)S(1)}, u32[]{:S(2)}, u32[]{:S(2)}) %collective-permute-start.9) | collective-permute-done | bytes 544 | tf_op jit(solution)/shard_map/ppermute | solution.py:261
  40.5 0.6 %fusion = (f32[1,1]{1,0:T(1,128)}, f32[1,1]{1,0:T(1,128)}) fusion(f32[1,128]{1,0:T(1,128)S(1)} %add_multiply_fusion), kind=kLoop, calls=%fused_computation.1 | loop fusion | bytes 16 | tf_op jit(solution)/shard_map/slice | solution.py:379
  (12 shorter events, 0.0 us)
Async XLA Ops:
  1.6 9.6 %collective-permute-start.2 = (f32[48,128]{1,0:T(8,128)S(1)}, f32[48,128]{1,0:T(8,128)S(1)}, u32[]{:S(2)}, u32[]{:S(2)}) collective-permute-start(f32[48,128]{1,0:T(8,128)S(1)} %get-tuple-element.12.own), channel_id=1, source_target_pairs={{4,0},{8,4},{12,8},{0,12},{5,1},{9,5},{13,9},{1,13},{6,2},{10,6},{... | collective-permute-start | bytes 73736 | tf_op jit(solution)/shard_map/ppermute | solution.py:306
  6.7 5.6 %collective-permute-start.1 = (f32[48,128]{1,0:T(8,128)S(1)}, f32[48,128]{1,0:T(8,128)S(1)}, u32[]{:S(2)}, u32[]{:S(2)}) collective-permute-start(f32[48,128]{1,0:T(8,128)S(1)} %get-tuple-element.12.own), channel_id=1, source_target_pairs={{12,0},{0,4},{4,8},{8,12},{13,1},{1,5},{5,9},{9,13},{14,2},{2,6},{... | collective-permute-start | bytes 73736 | tf_op jit(solution)/shard_map/ppermute | solution.py:305
  6.7 4.5 %collective-permute-start = (f32[8,128]{1,0:T(8,128)S(1)}, f32[8,128]{1,0:T(8,128)S(1)}, u32[]{:S(2)}, u32[]{:S(2)}) collective-permute-start(f32[8,128]{1,0:T(8,128)S(1)} %get-tuple-element.11), channel_id=1, source_target_pairs={{8,0},{12,4},{0,8},{4,12},{9,1},{13,5},{1,9},{5,13},{10,2},{14,6},... | collective-permute-start | bytes 12296 | tf_op jit(solution)/shard_map/ppermute | solution.py:307
  12.7 5.5 %collective-permute-start.5 = (f32[96,128]{1,0:T(8,128)S(1)}, f32[96,128]{1,0:T(8,128)S(1)}, u32[]{:S(2)}, u32[]{:S(2)}) collective-permute-start(f32[96,128]{1,0:T(8,128)S(1)} %migrate.1.moved.refs_0_), channel_id=1, source_target_pairs={{1,0},{0,1},{3,2},{2,3},{5,4},{4,5},{7,6},{6,7},{9,8},{8,9},{11,10... | collective-permute-start | bytes 147464 | tf_op jit(solution)/shard_map/ppermute | solution.py:326
  12.8 5.5 %collective-permute-start.4 = (f32[96,128]{1,0:T(8,128)S(1)}, f32[96,128]{1,0:T(8,128)S(1)}, u32[]{:S(2)}, u32[]{:S(2)}) collective-permute-start(f32[96,128]{1,0:T(8,128)S(1)} %migrate.1.moved.refs_0_), channel_id=1, source_target_pairs={{2,0},{3,1},{0,2},{1,3},{6,4},{7,5},{4,6},{5,7},{10,8},{11,9},{8,1... | collective-permute-start | bytes 147464 | tf_op jit(solution)/shard_map/ppermute | solution.py:326
  14.3 3.9 %collective-permute-start.3 = (f32[96,128]{1,0:T(8,128)S(1)}, f32[96,128]{1,0:T(8,128)S(1)}, u32[]{:S(2)}, u32[]{:S(2)}) collective-permute-start(f32[96,128]{1,0:T(8,128)S(1)} %migrate.1.moved.refs_0_), channel_id=1, source_target_pairs={{3,0},{2,1},{1,2},{0,3},{7,4},{6,5},{5,6},{4,7},{11,8},{10,9},{9,1... | collective-permute-start | bytes 147464 | tf_op jit(solution)/shard_map/ppermute | solution.py:326
  16.0 0.7 %copy-start = (f32[3]{0:T(128)S(1)}, f32[3]{0:T(128)}, u32[]{:S(2)}) copy-start(f32[3]{0:T(128)} %edge.3) | copy-start | bytes 40
  18.2 0.7 %copy-start.1 = (s32[1,1,1,6]{3,2,1,0:T(1,128)S(1)}, s32[1,1,1,6]{3,2,1,0:T(1,128)}, u32[]{:S(2)}) copy-start(s32[1,1,1,6]{3,2,1,0:T(1,128)} %param.16) | copy-start | bytes 76
  25.1 1.8 %collective-permute-start.6 = (f32[1,128]{1,0:T(1,128)S(1)}, f32[1,128]{1,0:T(1,128)S(1)}, u32[]{:S(2)}, u32[]{:S(2)}) collective-permute-start(f32[1,128]{1,0:T(1,128)S(1)} %get-tuple-element.16), channel_id=1, source_target_pairs={{0,1},{1,0},{2,3},{3,2},{4,5},{5,4},{6,7},{7,6},{8,9},{9,8},{10,11... | collective-permute-start | bytes 1544 | tf_op jit(solution)/shard_map/ppermute | solution.py:261
  27.0 5.5 %collective-permute-start.7 = (f32[1,128]{1,0:T(1,128)S(1)}, f32[1,128]{1,0:T(1,128)S(1)}, u32[]{:S(2)}, u32[]{:S(2)}) collective-permute-start(f32[1,128]{1,0:T(1,128)S(1)} %add.12), channel_id=1, source_target_pairs={{0,2},{2,0},{1,3},{3,1},{4,6},{6,4},{5,7},{7,5},{8,10},{10,8},{9,1... | collective-permute-start | bytes 1544 | tf_op jit(solution)/shard_map/ppermute | solution.py:261
  32.5 3.6 %collective-permute-start.8 = (f32[1,128]{1,0:T(1,128)S(1)}, f32[1,128]{1,0:T(1,128)S(1)}, u32[]{:S(2)}, u32[]{:S(2)}) collective-permute-start(f32[1,128]{1,0:T(1,128)S(1)} %add.13), channel_id=1, source_target_pairs={{0,4},{4,0},{8,12},{12,8},{1,5},{5,1},{9,13},{13,9},{2,6},{6,2},{1... | collective-permute-start | bytes 1544 | tf_op jit(solution)/shard_map/ppermute | solution.py:261
  36.1 4.5 %collective-permute-start.9 = (f32[1,128]{1,0:T(1,128)S(1)}, f32[1,128]{1,0:T(1,128)S(1)}, u32[]{:S(2)}, u32[]{:S(2)}) collective-permute-start(f32[1,128]{1,0:T(1,128)S(1)} %add.14), channel_id=1, source_target_pairs={{0,8},{4,12},{8,0},{12,4},{1,9},{5,13},{9,1},{13,5},{2,10},{6,14},... | collective-permute-start | bytes 1544 | tf_op jit(solution)/shard_map/ppermute | solution.py:261
